TPU v7x, 256 devices: a whole 4x4x8 slice. The times are simulated.
256 devices in a mesh: lat: 16 (over y, x_hi, core), lon: 16 (over x_lo, z).
Axes of the slice: x: 4 (x_hi: 2, x_lo: 2; x = x_hi * 2 + x_lo), y: 4, z: 8, core: 2. Of those that a mesh axis runs over, the one named last changes fastest.
Arguments:
- inputs: bfloat16 [256, 1536, 256], P('lat', 'lon'), may hold values from -6 to 6
- first_filter: bfloat16 [3, 3, 256, 256], replicated, may hold values from -0.125 to 0.125
- second_filter: bfloat16 [3, 3, 256, 256], replicated, may hold values from -0.125 to 0.125
- cotangent: bfloat16 [256, 1536, 256], P('lat', 'lon'), may hold values from -30 to 30
Outputs:
- input_grad: bfloat16 [256, 1536, 256], P('lat', 'lon')
- first_grad: float32 [3, 3, 256, 256], replicated
- second_grad: float32 [3, 3, 256, 256], replicated
All inputs are finite; a program needn't handle non-finite values.
Results may differ from a plain program's by a relative error of at most 0.0061.
Values may be sent and summed in bfloat16 or wider, within the bound.
A program may use at most 64 MiB of HBM per device.

v0:
```python
import jax
import jax.numpy as jnp
from jax import lax
from jax.sharding import PartitionSpec as P


def extended(block, sides, width):
    for axis, dim in sides:
        count = lax.axis_size(axis)
        forward = [(i, i + 1) for i in range(count - 1)]
        forward.append((count - 1, 0))
        backward = [(target, source) for source, target in forward]
        low = lax.ppermute(
            lax.slice_in_dim(block, block.shape[dim] - width, None, axis=dim), axis, forward
        )
        high = lax.ppermute(lax.slice_in_dim(block, 0, width, axis=dim), axis, backward)
        block = jnp.concatenate([low, block, high], axis=dim)
    return block


def mask_rows(padded, width):
    rows = padded.shape[0] - 2 * width
    position = lax.broadcasted_iota(jnp.int32, (padded.shape[0], 1, 1), 0)
    index = lax.axis_index("lat")
    count = lax.axis_size("lat")
    dropped = (position < width) & (index == 0) | (position >= rows + width) & (index == count - 1)
    return jnp.where(dropped, jnp.zeros((), padded.dtype), padded)


def extend(field):
    padded = extended(field, (("lat", 0), ("lon", 1)), 1)
    return mask_rows(padded, 1)


def conv_taps(padded, weight, rows, cols, flipped):
    total = jnp.zeros(
        (rows * cols, weight.shape[3] if not flipped else weight.shape[2]), jnp.float32
    )
    for first in range(3):
        for second in range(3):
            piece = padded[first : first + rows, second : second + cols, :].reshape(rows * cols, -1)
            if flipped:
                total = total + lax.dot_general(
                    piece,
                    weight[2 - first, 2 - second],
                    (((1,), (1,)), ((), ())),
                    preferred_element_type=jnp.float32,
                )
            else:
                total = total + jnp.dot(
                    piece, weight[first, second], preferred_element_type=jnp.float32
                )
    return total.reshape(rows, cols, -1)


def filter_grad(padded, delta, rows, cols):
    flat = delta.reshape(rows * cols, -1)
    taps = []
    for first in range(3):
        for second in range(3):
            piece = padded[first : first + rows, second : second + cols, :].reshape(rows * cols, -1)
            taps.append(
                lax.dot_general(
                    piece, flat, (((0,), (0,)), ((), ())), preferred_element_type=jnp.float32
                )
            )
    return jnp.stack(taps).reshape(3, 3, flat.shape[1], flat.shape[1])


def gelu_value(value):
    return value * 0.5 * (1.0 + jax.scipy.special.erf(value * 0.7071067811865476))


def gelu_slope(value):
    return (
        0.5 * (1.0 + jax.scipy.special.erf(value * 0.7071067811865476))
        + value * jnp.exp(-0.5 * value * value) * 0.3989422804014327
    )


def body(inputs, first_filter, second_filter, cotangent):
    rows, cols = (inputs.shape[0], inputs.shape[1])
    padded_in = extend(inputs)
    hidden_one = conv_taps(padded_in, first_filter, rows, cols, False)
    act = gelu_value(hidden_one).astype(jnp.bfloat16)
    padded_act = extend(act)
    hidden_two = conv_taps(padded_act, second_filter, rows, cols, False)
    delta_two = (cotangent.astype(jnp.float32) * gelu_slope(hidden_two)).astype(jnp.bfloat16)
    second_part = filter_grad(padded_act, delta_two, rows, cols)
    act_grad = conv_taps(extend(delta_two), second_filter, rows, cols, True)
    delta_one = (act_grad * gelu_slope(hidden_one)).astype(jnp.bfloat16)
    first_part = filter_grad(padded_in, delta_one, rows, cols)
    first_grad, second_grad = lax.psum((first_part, second_part), ("lat", "lon"))
    input_grad = conv_taps(extend(delta_one), first_filter, rows, cols, True).astype(jnp.bfloat16)
    return (input_grad, first_grad, second_grad)


def solution(mesh):
    in_specs = (P("lat", "lon", None), P(), P(), P("lat", "lon", None))
    out_specs = (P("lat", "lon", None), P(), P())
    return jax.shard_map(body, mesh=mesh, in_specs=in_specs, out_specs=out_specs, check_vma=False)
```

profile of v0, /device:TPU:1, one launch (start us, length us, event | category | flops | bytes accessed | tf_op | source)
XLA Modules:
  0.0 366.4 jit_solution(177461042161218272)
XLA Ops:
  7.2 0.8 fusion.133
  8.0 4.2 %collective-permute-start = (bf16[1,96,256]{2,1,0:T(8,128)(2,1)S(1)}, bf16[1,96,256]{2,1,0:T(8,128)(2,1)S(1)}, u32[]{:S(2)}, u32[]{:S(2)}) collective-permute-start(bf16[1,96,256]{2,1,0:T(8,128)(2,1)S(1)} %get-tuple-element.56), channel_id=1, source_target_pairs={{0,16},{16,32},{32,48},{48,64},{64,80},{80,96},{96,112},{112,128},... | collective-permute-start | bytes 147464 | tf_op jit(solution)/shard_map/ppermute | solution.py:13
  12.2 1.2 collective-permute-done
  13.4 1.2 constant_dynamic-update-slice_fusion.1
  14.6 2.9 collective-permute-done.1
  17.6 5.4 %collective-permute-start.3 = (bf16[18,1,256]{2,1,0:T(2,128)(2,1)S(1)}, bf16[18,1,256]{2,1,0:T(2,128)(2,1)S(1)}, u32[]{:S(2)}, u32[]{:S(2)}) collective-permute-start(bf16[18,1,256]{2,1,0:T(2,128)(2,1)S(1)} %get-tuple-element.48), channel_id=1, source_target_pairs={{1,0},{2,1},{3,2},{4,3},{5,4},{6,5},{7,6},{8,7},{9,8},{10,9},{11,1... | collective-permute-start | bytes 27656 | tf_op jit(solution)/shard_map/ppermute | solution.py:16
  23.0 0.9 collective-permute-done.3
  23.9 3.8 %collective-permute-done.2 = bf16[18,1,256]{2,1,0:T(2,128)(2,1)S(1)} collective-permute-done((bf16[18,1,256]{2,1,0:T(2,128)(2,1)S(1)}, bf16[18,1,256]{2,1,0:T(2,128)(2,1)S(1)}, u32[]{:S(2)}, u32[]{:S(2)}) %collective-permute-start.2) | collective-permute-done | bytes 9248 | tf_op jit(solution)/shard_map/ppermute | solution.py:13
  27.7 0.6 maximum_select_fusion
  28.3 0.8 fusion.128
  29.1 0.4 copy-done.1
  33.2 3.1 collective-permute-start.5
  36.6 1.7 collective-permute-done.5
  38.3 2.0 collective-permute-done.4
  40.5 1.5 collective-permute-start.6
  41.9 1.1 collective-permute-done.7
  43.1 2.7 collective-permute-done.6
  45.8 0.6 maximum_select_fusion.1
  46.3 1.1 fusion.127
  50.9 0.7 copy-done.5
  51.7 0.7 fusion.6
  52.8 7.3 %collective-permute-start.9 = (bf16[1,96,256]{2,1,0:T(8,128)(2,1)S(1)}, bf16[1,96,256]{2,1,0:T(8,128)(2,1)S(1)}, u32[]{:S(2)}, u32[]{:S(2)}) collective-permute-start(bf16[1,96,256]{2,1,0:T(8,128)(2,1)S(1)} %get-tuple-element.52), channel_id=1, source_target_pairs={{16,0},{32,16},{48,32},{64,48},{80,64},{96,80},{112,96},{128,112},... | collective-permute-start | bytes 147464 | tf_op jit(solution)/shard_map/ppermute | solution.py:16
  60.2 0.4 fusion.20
  60.6 0.4 fusion.19
  61.0 0.4 fusion.18
  61.4 0.4 fusion.17
  61.9 0.4 fusion.16
  62.7 0.4 fusion.14
  63.3 1.5 collective-permute-start.10
  64.8 0.4 fusion.13
  65.2 1.0 collective-permute-done.11
  66.2 2.1 collective-permute-done.10
  68.3 0.6 maximum_select_fusion.2
  68.9 1.1 fusion.126
  73.6 0.7 fusion.12
  74.7 5.4 %collective-permute-start.13 = (bf16[1,96,256]{2,1,0:T(8,128)(2,1)S(1)}, bf16[1,96,256]{2,1,0:T(8,128)(2,1)S(1)}, u32[]{:S(2)}, u32[]{:S(2)}) collective-permute-start(bf16[1,96,256]{2,1,0:T(8,128)(2,1)S(1)} %get-tuple-element.50), channel_id=1, source_target_pairs={{16,0},{32,16},{48,32},{64,48},{80,64},{96,80},{112,96},{128,112},... | collective-permute-start | bytes 147464 | tf_op jit(solution)/shard_map/ppermute | solution.py:16
  80.5 0.4 fusion.28
  81.4 0.4 fusion.26
  82.7 0.4 fusion.23
  83.3 1.5 collective-permute-start.14
  85.1 1.4 copy-done.4
  86.6 1.7 collective-permute-done.14
  88.3 0.6 maximum_select_fusion.3
  88.9 1.1 fusion.125
  93.2 1.3 fusion
  94.5 260.3 %all-reduce.3.cloned.1.call-done = (f32[3,3,256,256]{3,2,1,0:T(8,128)}, f32[3,3,256,256]{3,2,1,0:T(8,128)}) async-done(((f32[3,3,256,256]{3,2,1,0:T(8,128)}, f32[3,3,256,256]{3,2,1,0:T(8,128)}), (f32[3,3,256,256]{3,2,1,0:T(8,128)}, f32[3,3,256,256]{3,2,1,0:T(8,128)})) %all-reduce.3.cloned.1.call-update) | async-done | bytes 4718608 | tf_op jit(solution)/shard_map/psum | solution.py:93
  354.8 3.4 copy.27
  358.2 1.4 copy.28
  (78 shorter events, 18.0 us)
Async XLA Ops:
  7.2 347.6 %all-reduce.3.cloned.1.call-start = ((), (), s32[]{:S(2)}) async-start(), calls=%async_computation | async-start | bytes 9437184 | tf_op jit(solution)/shard_map/psum | solution.py:93
  8.0 5.4 %collective-permute-start = (bf16[1,96,256]{2,1,0:T(8,128)(2,1)S(1)}, bf16[1,96,256]{2,1,0:T(8,128)(2,1)S(1)}, u32[]{:S(2)}, u32[]{:S(2)}) collective-permute-start(bf16[1,96,256]{2,1,0:T(8,128)(2,1)S(1)} %get-tuple-element.56), channel_id=1, source_target_pairs={{0,16},{16,32},{32,48},{48,64},{64,80},{80,96},{96,112},{112,128},... | collective-permute-start | bytes 147464 | tf_op jit(solution)/shard_map/ppermute | solution.py:13
  12.2 5.3 %collective-permute-start.1 = (bf16[1,96,256]{2,1,0:T(8,128)(2,1)S(1)}, bf16[1,96,256]{2,1,0:T(8,128)(2,1)S(1)}, u32[]{:S(2)}, u32[]{:S(2)}) collective-permute-start(bf16[1,96,256]{2,1,0:T(8,128)(2,1)S(1)} %get-tuple-element.55), channel_id=1, source_target_pairs={{16,0},{32,16},{48,32},{64,48},{80,64},{96,80},{112,96},{128,112},... | collective-permute-start | bytes 147464 | tf_op jit(solution)/shard_map/ppermute | solution.py:16
  17.6 6.3 %collective-permute-start.3 = (bf16[18,1,256]{2,1,0:T(2,128)(2,1)S(1)}, bf16[18,1,256]{2,1,0:T(2,128)(2,1)S(1)}, u32[]{:S(2)}, u32[]{:S(2)}) collective-permute-start(bf16[18,1,256]{2,1,0:T(2,128)(2,1)S(1)} %get-tuple-element.48), channel_id=1, source_target_pairs={{1,0},{2,1},{3,2},{4,3},{5,4},{6,5},{7,6},{8,7},{9,8},{10,9},{11,1... | collective-permute-start | bytes 27656 | tf_op jit(solution)/shard_map/ppermute | solution.py:16
  23.0 4.7 %collective-permute-start.2 = (bf16[18,1,256]{2,1,0:T(2,128)(2,1)S(1)}, bf16[18,1,256]{2,1,0:T(2,128)(2,1)S(1)}, u32[]{:S(2)}, u32[]{:S(2)}) collective-permute-start(bf16[18,1,256]{2,1,0:T(2,128)(2,1)S(1)} %get-tuple-element.47), channel_id=1, source_target_pairs={{0,1},{1,2},{2,3},{3,4},{4,5},{5,6},{6,7},{7,8},{8,9},{9,10},{10,1... | collective-permute-start | bytes 27656 | tf_op jit(solution)/shard_map/ppermute | solution.py:13
  28.3 1.3 copy-start.1
  33.2 5.1 %collective-permute-start.5 = (bf16[1,96,256]{2,1,0:T(8,128)(2,1)S(1)}, bf16[1,96,256]{2,1,0:T(8,128)(2,1)S(1)}, u32[]{:S(2)}, u32[]{:S(2)}) collective-permute-start(bf16[1,96,256]{2,1,0:T(8,128)(2,1)S(1)} %get-tuple-element.54), channel_id=1, source_target_pairs={{16,0},{32,16},{48,32},{64,48},{80,64},{96,80},{112,96},{128,112},... | collective-permute-start | bytes 147464 | tf_op jit(solution)/shard_map/ppermute | solution.py:16
  36.3 4.0 %collective-permute-start.4 = (bf16[1,96,256]{2,1,0:T(8,128)(2,1)S(1)}, bf16[1,96,256]{2,1,0:T(8,128)(2,1)S(1)}, u32[]{:S(2)}, u32[]{:S(2)}) collective-permute-start(bf16[1,96,256]{2,1,0:T(8,128)(2,1)S(1)} %get-tuple-element.53), channel_id=1, source_target_pairs={{0,16},{16,32},{32,48},{48,64},{64,80},{80,96},{96,112},{112,128},... | collective-permute-start | bytes 147464 | tf_op jit(solution)/shard_map/ppermute | solution.py:13
  40.4 2.7 collective-permute-start.7
  40.5 5.3 %collective-permute-start.6 = (bf16[18,1,256]{2,1,0:T(2,128)(2,1)S(1)}, bf16[18,1,256]{2,1,0:T(2,128)(2,1)S(1)}, u32[]{:S(2)}, u32[]{:S(2)}) collective-permute-start(bf16[18,1,256]{2,1,0:T(2,128)(2,1)S(1)} %get-tuple-element.45), channel_id=1, source_target_pairs={{0,1},{1,2},{2,3},{3,4},{4,5},{5,6},{6,7},{7,8},{8,9},{9,10},{10,1... | collective-permute-start | bytes 27656 | tf_op jit(solution)/shard_map/ppermute | solution.py:13
  46.3 1.3 copy-start
  50.5 1.1 copy-start.5
  52.8 10.4 %collective-permute-start.9 = (bf16[1,96,256]{2,1,0:T(8,128)(2,1)S(1)}, bf16[1,96,256]{2,1,0:T(8,128)(2,1)S(1)}, u32[]{:S(2)}, u32[]{:S(2)}) collective-permute-start(bf16[1,96,256]{2,1,0:T(8,128)(2,1)S(1)} %get-tuple-element.52), channel_id=1, source_target_pairs={{16,0},{32,16},{48,32},{64,48},{80,64},{96,80},{112,96},{128,112},... | collective-permute-start | bytes 147464 | tf_op jit(solution)/shard_map/ppermute | solution.py:16
  60.2 3.0 collective-permute-start.8
  63.2 3.0 collective-permute-start.11
  63.3 5.0 %collective-permute-start.10 = (bf16[18,1,256]{2,1,0:T(2,128)(2,1)S(1)}, bf16[18,1,256]{2,1,0:T(2,128)(2,1)S(1)}, u32[]{:S(2)}, u32[]{:S(2)}) collective-permute-start(bf16[18,1,256]{2,1,0:T(2,128)(2,1)S(1)} %get-tuple-element.43), channel_id=1, source_target_pairs={{0,1},{1,2},{2,3},{3,4},{4,5},{5,6},{6,7},{7,8},{8,9},{9,10},{10,1... | collective-permute-start | bytes 27656 | tf_op jit(solution)/shard_map/ppermute | solution.py:13
  65.2 4.8 %copy-start.3 = (f32[9,256,256]{2,1,0:T(8,128)}, f32[9,256,256]{2,1,0:T(8,128)S(1)}, u32[]{:S(2)}) copy-start(f32[9,256,256]{2,1,0:T(8,128)S(1)} %fusion.13) | copy-start | bytes 7077892
  74.7 8.4 %collective-permute-start.13 = (bf16[1,96,256]{2,1,0:T(8,128)(2,1)S(1)}, bf16[1,96,256]{2,1,0:T(8,128)(2,1)S(1)}, u32[]{:S(2)}, u32[]{:S(2)}) collective-permute-start(bf16[1,96,256]{2,1,0:T(8,128)(2,1)S(1)} %get-tuple-element.50), channel_id=1, source_target_pairs={{16,0},{32,16},{48,32},{64,48},{80,64},{96,80},{112,96},{128,112},... | collective-permute-start | bytes 147464 | tf_op jit(solution)/shard_map/ppermute | solution.py:16
  80.1 3.0 collective-permute-start.12
  83.2 3.4 collective-permute-start.15
  83.3 5.1 %collective-permute-start.14 = (bf16[18,1,256]{2,1,0:T(2,128)(2,1)S(1)}, bf16[18,1,256]{2,1,0:T(2,128)(2,1)S(1)}, u32[]{:S(2)}, u32[]{:S(2)}) collective-permute-start(bf16[18,1,256]{2,1,0:T(2,128)(2,1)S(1)} %get-tuple-element.41), channel_id=1, source_target_pairs={{0,1},{1,2},{2,3},{3,4},{4,5},{5,6},{6,7},{7,8},{8,9},{9,10},{10,1... | collective-permute-start | bytes 27656 | tf_op jit(solution)/shard_map/ppermute | solution.py:13
  85.1 1.4 copy-start.4
  354.8 3.4 copy-start.2
Sparse Core Ops, SparseCore 0:
  86.7 268.0 all-reduce.2
where the time goes:
time: 368 us; the launch traced here: 366 us
  waiting for transfers between devices  282 us (77%)
  starting transfers between devices  30.4 us (8%)
  matrix products  22.2 us (6%)
  between operations  14.6 us (4%)
  local copies, waits for them, and re-layouts  13.6 us (4%)
  other arithmetic  4.03 us (1%)
    psum x1, waiting for transfers between devices, body(): lax.psum((first_part, second_part), ('lat', 'lon'))  260 us
    ppermute x8, starting transfers between devices, extended(): lax.ppermute(lax.slice_in_dim(block, 0, width, axis=dim), axis, backward)  21.5 us
    ppermute x8, waiting for transfers between devices, extended(): lax.ppermute(lax.slice_in_dim(block, block.shape[dim] - width, None, axis...  13.6 us
    ppermute x8, starting transfers between devices, extended(): lax.ppermute(lax.slice_in_dim(block, block.shape[dim] - width, None, axis...  8.86 us
    unnamed x16, local copies, waits for them, and re-layouts  8.77 us
    dot_general x18, matrix products, conv_taps(): lax.dot_general(piece, weight[2 - first, 2 - second], (((1,), (1,)), ((),...  8.1 us
    ppermute x8, waiting for transfers between devices, extended(): lax.ppermute(lax.slice_in_dim(block, 0, width, axis=dim), axis, backward)  7.65 us
    dot_general x18, matrix products, filter_grad(): lax.dot_general(piece, flat, (((0,), (0,)), ((), ())), preferred_element_...  7.52 us
  transfers between devices with their start and end apart: 17, of which 12 were waited for; matrix products, arithmetic and copies ran while one was open for 4% of the time, Pallas kernels for 0%

commit v1 on v0

v1 whole, which is shorter than its diff:
```python
import functools

import jax
import jax.numpy as jnp
from jax import lax
from jax.experimental import pallas as pl
from jax.experimental.pallas import tpu as pltpu
from jax.sharding import PartitionSpec as P

MESH = pl.DeviceIdType.MESH
F32 = jnp.float32
BF16 = jnp.bfloat16
VMEM_LIMIT = 60 * 1024 * 1024


def slope_parts(value):
    half = 0.5 * (1.0 + lax.erf(value * 0.7071067811865476))
    slope = half + value * jnp.exp(-0.5 * value * value) * 0.3989422804014327
    return half, slope


def stage_kernel(
    lats, lons, rows, cols, ch, group,
    in_ref, w1_ref, w2_ref, cot_ref,
    dx_ref, g1_ref, g2_ref,
    xs, acts, d2s, d1s, slope1, turned, edge, sent, got, halo, send_sem, recv_sem,
):
    lat, lon = lax.axis_index("lat"), lax.axis_index("lon")
    size = group * cols
    blocks = rows // group

    def spot(dlat, dlon):
        return {"lat": lax.rem(lat + dlat + lats, lats), "lon": lax.rem(lon + dlon + lons, lons)}

    barrier = pltpu.get_barrier_semaphore()
    for dlat in (-1, 0, 1):
        for dlon in (-1, 0, 1):
            if dlat or dlon:
                pl.semaphore_signal(barrier, inc=1, device_id=spot(dlat, dlon), device_id_type=MESH)
    pl.semaphore_wait(barrier, 8)

    def line(row):
        return pl.ds(pl.multiple_of(row * cols, cols), cols)

    def put_row(field, row, value):
        where = line(row)
        field[where, ch : 2 * ch] = value.astype(BF16)
        field[where, 0:ch] = pltpu.roll(value, 1, 0).astype(BF16)
        field[where, 2 * ch : 3 * ch] = pltpu.roll(value, cols - 1, 0).astype(BF16)
        edge[0, pl.ds(row - 1, 1), :] = value[0:1]
        edge[1, pl.ds(row - 1, 1), :] = value[cols - 1 : cols]

    def copies(index, field):
        mid = slice(ch, 2 * ch)
        plan = [
            (field.at[cols : 2 * cols, mid], field.at[(rows + 1) * cols : (rows + 2) * cols, mid], (-1, 0)),
            (field.at[rows * cols : (rows + 1) * cols, mid], field.at[0:cols, mid], (1, 0)),
        ]
        for dlat in (-1, 0, 1):
            plan.append((sent.at[index, 0], got.at[index, 1, 1 - dlat], (dlat, -1)))
            plan.append((sent.at[index, 1], got.at[index, 0, 1 - dlat], (dlat, 1)))
        return [
            pltpu.make_async_remote_copy(
                src_ref=src, dst_ref=dst,
                send_sem=send_sem.at[index, n], recv_sem=recv_sem.at[index, n],
                device_id=spot(*shift), device_id_type=MESH,
            )
            for n, (src, dst, shift) in enumerate(plan)
        ]

    def send(index, field):
        for side in range(2):
            sent[index, side] = edge[side].astype(BF16)
        for copy in copies(index, field):
            copy.start()

    up, down = lat > 0, lat < lats - 1

    def receive(index, field):
        for copy in copies(index, field):
            copy.wait()
        for side in range(2):
            halo[side, 8 : 8 + rows] = got[index, side, 1].astype(F32)
            halo[side, 7:8] = jnp.where(up, got[index, side, 0].astype(F32)[rows - 1 : rows], 0.0)
            halo[side, 8 + rows : 9 + rows] = jnp.where(down, got[index, side, 2].astype(F32)[0:1], 0.0)
        spots = lax.broadcasted_iota(jnp.int32, (16, ch), 0)

        def fix(row, carry):
            base = pl.multiple_of(row * cols, cols)
            head = pl.ds(base, 16)
            tail = pl.ds(pl.multiple_of(base + cols - 16, 16), 16)
            left = halo[0, pl.ds(7 + row, 1), :]
            right = halo[1, pl.ds(7 + row, 1), :]
            field[head, 0:ch] = jnp.where(spots == 0, left, field[head, 0:ch].astype(F32)).astype(BF16)
            field[tail, 2 * ch : 3 * ch] = jnp.where(
                spots == 15, right, field[tail, 2 * ch : 3 * ch].astype(F32)
            ).astype(BF16)
            return carry

        lax.fori_loop(1, rows + 1, fix, 0)
        place = lax.broadcasted_iota(jnp.int32, (cols, ch), 0)
        for row, valid in ((0, up), (rows + 1, down)):
            where = slice(row * cols, (row + 1) * cols)
            value = jnp.where(valid, field[where, ch : 2 * ch].astype(F32), 0.0)
            field[where, ch : 2 * ch] = value.astype(BF16)
            field[where, 0:ch] = jnp.where(
                place == 0, halo[0, 7 + row : 8 + row, :], pltpu.roll(value, 1, 0)
            ).astype(BF16)
            field[where, 2 * ch : 3 * ch] = jnp.where(
                place == cols - 1, halo[1, 7 + row : 8 + row, :], pltpu.roll(value, cols - 1, 0)
            ).astype(BF16)

    def conv(field, weight, block):
        total = None
        for a in range(3):
            piece = field[pl.ds(pl.multiple_of((block * group + a) * cols, cols), size), :]
            part = jnp.dot(piece, weight[a], preferred_element_type=F32)
            total = part if total is None else total + part
        return total

    def conv_t(field, weight, block):
        total = None
        for a in range(3):
            for b in range(3):
                piece = field[
                    pl.ds(pl.multiple_of((block * group + a) * cols, cols), size), b * ch : (b + 1) * ch
                ]
                part = lax.dot_general(
                    piece, weight[2 - a, (2 - b) * ch : (3 - b) * ch, :],
                    (((1,), (1,)), ((), ())), preferred_element_type=F32,
                )
                total = part if total is None else total + part
        return total

    def put_block(field, block, value):
        for k in range(group):
            put_row(field, block * group + 1 + k, value[k * cols : (k + 1) * cols])

    def filter_grad(field, grad):
        def tap(a, carry):
            grad[a] = jnp.dot(
                turned[...], field[pl.ds(pl.multiple_of(a * cols, cols), rows * cols), :],
                preferred_element_type=F32,
            )
            return carry

        lax.fori_loop(0, 3, tap, 0)

    def load(row, carry):
        put_row(xs, row + 1, in_ref[row].astype(F32))
        return carry

    lax.fori_loop(0, rows, load, 0)
    send(0, xs)
    receive(0, xs)

    def first(block, carry):
        value = conv(xs, w1_ref, block)
        half, slope = slope_parts(value)
        slope1[pl.ds(pl.multiple_of(block * size, size), size), :] = slope
        put_block(acts, block, value * half)
        return carry

    lax.fori_loop(0, blocks, first, 0)
    send(1, acts)
    receive(1, acts)

    def second(block, carry):
        value = conv(acts, w2_ref, block)
        _, slope = slope_parts(value)
        rate = cot_ref[pl.ds(block * group, group)].astype(F32).reshape(size, ch)
        delta = rate * slope
        put_block(d2s, block, delta)
        turned[:, pl.ds(pl.multiple_of(block * size, size), size)] = delta.T.astype(BF16)
        return carry

    lax.fori_loop(0, blocks, second, 0)
    send(2, d2s)
    filter_grad(acts, g2_ref)
    receive(2, d2s)

    def third(block, carry):
        value = conv_t(d2s, w2_ref, block)
        delta = value * slope1[pl.ds(pl.multiple_of(block * size, size), size), :]
        put_block(d1s, block, delta)
        turned[:, pl.ds(pl.multiple_of(block * size, size), size)] = delta.T.astype(BF16)
        return carry

    lax.fori_loop(0, blocks, third, 0)
    send(3, d1s)
    filter_grad(xs, g1_ref)
    receive(3, d1s)

    def fourth(block, carry):
        value = conv_t(d1s, w1_ref, block)
        dx_ref[pl.ds(block * group, group)] = value.astype(BF16).reshape(group, cols, ch)
        return carry

    lax.fori_loop(0, blocks, fourth, 0)


def reduce_kernel(
    ch, half,
    g1_ref, g2_ref, o1_ref, o2_ref,
    pair, mine, out1, in1, mine2, out2, in2, mine3, in3, final,
    pair_send, pair_recv, s1, r1, s2, r2, s3, r3, s4, r4, s5, r5, s6, r6, last_send, last_recv,
):
    lat, lon = lax.axis_index("lat"), lax.axis_index("lon")
    core = lax.rem(lat, 2)
    x = lax.rem(lat // 2, 2) * 2 + lon // 8
    y = lat // 4
    z = lax.rem(lon, 8)

    def at(x, y, z, core):
        return {"lat": y * 4 + (x // 2) * 2 + core, "lon": lax.rem(x, 2) * 8 + z}

    partner = at(x, y, z, 1 - core)

    def along_x(d):
        return at(lax.rem(x + d, 4), y, z, core)

    def along_y(d):
        return at(x, lax.rem(y + d, 4), z, core)

    def along_z(d):
        return at(x, y, lax.rem(z + d, 8), core)

    barrier = pltpu.get_barrier_semaphore()
    peers = [partner] + [along_x(d) for d in (1, 2, 3)] + [along_y(d) for d in (1, 2, 3)]
    peers += [along_z(d) for d in range(1, 8)]
    for peer in peers:
        pl.semaphore_signal(barrier, inc=1, device_id=peer, device_id_type=MESH)
    pl.semaphore_wait(barrier, len(peers))

    grads = (g1_ref, g2_ref)
    outs = (o1_ref, o2_ref)
    order = ((x, along_x, y, along_y), (y, along_y, x, along_x))

    def remote(src, dst, send_sem, recv_sem, device):
        return pltpu.make_async_remote_copy(
            src_ref=src, dst_ref=dst, send_sem=send_sem, recv_sem=recv_sem,
            device_id=device, device_id_type=MESH,
        )

    def rows64(index):
        return pl.ds(pl.multiple_of(index * 64, 64), 64)

    def rows16(index):
        return pl.ds(pl.multiple_of(index * 16, 16), 16)

    def pair_copy(g):
        other = pl.ds(pl.multiple_of((1 - core) * half, half), half)
        return remote(grads[g].at[:, other, :], pair.at[g], pair_send.at[g], pair_recv.at[g], partner)

    def first_copies(g):
        index, peer = order[g][:2]
        return [
            remote(
                out1.at[g, :, rows64(lax.rem(index + d, 4)), :], in1.at[g, d - 1],
                s1.at[g, d - 1], r1.at[g, d - 1], peer(d),
            )
            for d in (1, 2, 3)
        ]

    def second_copies(g):
        index, peer = order[g][2:]
        return [
            remote(
                out2.at[g, :, rows16(lax.rem(index + d, 4)), :], in2.at[g, d - 1],
                s2.at[g, d - 1], r2.at[g, d - 1], peer(d),
            )
            for d in (1, 2, 3)
        ]

    def third_copies(g):
        found = []
        for d in range(1, 8):
            found.append(
                remote(
                    mine3.at[g, lax.rem(z + d, 8)], in3.at[g, z, 0],
                    s3.at[g, d - 1, 0], r3.at[g, d - 1, 0], along_z(d),
                )
            )
            found.append(
                remote(
                    mine3.at[g, 8], in3.at[g, z, 1],
                    s3.at[g, d - 1, 1], r3.at[g, d - 1, 1], along_z(d),
                )
            )
        return found

    def chunk(g):
        return rows16(order[g][0] * 4 + order[g][2])

    def fourth_copies(g):
        place = final.at[g, core, z, chunk(g), :]
        return [
            remote(place, place, s4.at[g, d - 1], r4.at[g, d - 1], along_z(d)) for d in range(1, 8)
        ]

    def fifth_copies(g):
        place = final.at[g, core, :, chunk(g), :]
        return [
            remote(place, place, s5.at[g, d - 1], r5.at[g, d - 1], order[g][3](d)) for d in (1, 2, 3)
        ]

    def sixth_copies(g):
        place = final.at[g, core, :, rows64(order[g][0]), :]
        return [
            remote(place, place, s6.at[g, d - 1], r6.at[g, d - 1], order[g][1](d)) for d in (1, 2, 3)
        ]

    def last_copy(g):
        place = final.at[g, core]
        return remote(place, place, last_send.at[g], last_recv.at[g], partner)

    for g in range(2):
        pair_copy(g).start()
    for g in range(2):
        pair_copy(g).wait()
        own = pl.ds(pl.multiple_of(core * half, half), half)
        for b in range(3):
            def turn(a, carry):
                total = grads[g][a, own, b * ch : (b + 1) * ch] + pair[g, a, :, b * ch : (b + 1) * ch]
                total = total.T
                mine[g, a * 3 + b] = total
                out1[g, a * 3 + b] = total.astype(BF16)
                return carry

            lax.fori_loop(0, 3, turn, 0)
        for copy in first_copies(g):
            copy.start()
    for g in range(2):
        for copy in first_copies(g):
            copy.wait()

        def add_first(t, carry):
            total = mine[g, t, rows64(order[g][0]), :]
            for d in range(3):
                total = total + in1[g, d, t].astype(F32)
            mine2[g, t] = total
            out2[g, t] = total.astype(BF16)
            return carry

        lax.fori_loop(0, 9, add_first, 0)
        for copy in second_copies(g):
            copy.start()
    for g in range(2):
        for copy in second_copies(g):
            copy.wait()

        def add_second(t, carry):
            total = mine2[g, t, rows16(order[g][2]), :]
            for d in range(3):
                total = total + in2[g, d, t].astype(F32)
            mine3[g, t] = total
            return carry

        lax.fori_loop(0, 9, add_second, 0)
        in3[g, z, 0] = mine3[g, z]
        in3[g, z, 1] = mine3[g, 8]
        for copy in third_copies(g):
            copy.start()
    for g in range(2):
        for copy in third_copies(g):
            copy.wait()
        for k in range(2):
            total = in3[g, 0, k]
            for m in range(1, 8):
                total = total + in3[g, m, k]
            final[g, core, z if k == 0 else 8, chunk(g), :] = total.astype(BF16)
        for copy in fourth_copies(g):
            copy.start()
    for g in range(2):
        for copy in fourth_copies(g):
            copy.wait()
        for copy in fifth_copies(g):
            copy.start()
    for g in range(2):
        for copy in fifth_copies(g):
            copy.wait()
        for copy in sixth_copies(g):
            copy.start()
    for g in range(2):
        for copy in sixth_copies(g):
            copy.wait()
        last_copy(g).start()
    for g in range(2):
        last_copy(g).wait()

        def emit(t, carry):
            for c in range(2):
                outs[g][t, :, c * half : (c + 1) * half] = final[g, c, t].astype(F32)
            return carry

        lax.fori_loop(0, 9, emit, 0)


def body(lats, lons, inputs, first_filter, second_filter, cotangent):
    rows, cols, ch = inputs.shape
    group = 4
    vmem = pl.BlockSpec(memory_space=pltpu.VMEM)
    cells = rows * cols
    padded = pltpu.VMEM(((rows + 2) * cols, 3 * ch), BF16)
    dx, g1, g2 = pl.pallas_call(
        functools.partial(stage_kernel, lats, lons, rows, cols, ch, group),
        out_shape=(
            jax.ShapeDtypeStruct((rows, cols, ch), BF16),
            jax.ShapeDtypeStruct((3, ch, 3 * ch), F32),
            jax.ShapeDtypeStruct((3, ch, 3 * ch), F32),
        ),
        in_specs=[vmem] * 4,
        out_specs=(vmem,) * 3,
        scratch_shapes=[
            padded, padded, padded, padded,
            pltpu.VMEM((cells, ch), F32),
            pltpu.VMEM((ch, cells), BF16),
            pltpu.VMEM((2, rows, ch), F32),
            pltpu.VMEM((4, 2, rows, ch), BF16),
            pltpu.VMEM((4, 2, 3, rows, ch), BF16),
            pltpu.VMEM((2, 16 + rows, ch), F32),
            pltpu.SemaphoreType.DMA((4, 8)),
            pltpu.SemaphoreType.DMA((4, 8)),
        ],
        compiler_params=pltpu.CompilerParams(
            collective_id=0, has_side_effects=True, vmem_limit_bytes=VMEM_LIMIT
        ),
        name="stages",
    )(
        inputs,
        first_filter.reshape(3, 3 * ch, ch),
        second_filter.reshape(3, 3 * ch, ch),
        cotangent,
    )
    half = ch // 2
    dma = pltpu.SemaphoreType.DMA
    o1, o2 = pl.pallas_call(
        functools.partial(reduce_kernel, ch, half),
        out_shape=(jax.ShapeDtypeStruct((9, ch, ch), F32),) * 2,
        in_specs=[vmem] * 2,
        out_specs=(vmem,) * 2,
        scratch_shapes=[
            pltpu.VMEM((2, 3, half, 3 * ch), F32),
            pltpu.VMEM((2, 9, ch, half), F32),
            pltpu.VMEM((2, 9, ch, half), BF16),
            pltpu.VMEM((2, 3, 9, 64, half), BF16),
            pltpu.VMEM((2, 9, 64, half), F32),
            pltpu.VMEM((2, 9, 64, half), BF16),
            pltpu.VMEM((2, 3, 9, 16, half), BF16),
            pltpu.VMEM((2, 9, 16, half), F32),
            pltpu.VMEM((2, 8, 2, 16, half), F32),
            pltpu.VMEM((2, 2, 9, ch, half), BF16),
            dma((2,)), dma((2,)),
            dma((2, 3)), dma((2, 3)),
            dma((2, 3)), dma((2, 3)),
            dma((2, 7, 2)), dma((2, 7, 2)),
            dma((2, 7)), dma((2, 7)),
            dma((2, 3)), dma((2, 3)),
            dma((2, 3)), dma((2, 3)),
            dma((2,)), dma((2,)),
        ],
        compiler_params=pltpu.CompilerParams(
            collective_id=1, has_side_effects=True, vmem_limit_bytes=VMEM_LIMIT
        ),
        name="reduce",
    )(g1, g2)
    return dx, o1.reshape(3, 3, ch, ch), o2.reshape(3, 3, ch, ch)


def solution(mesh):
    in_specs = (P("lat", "lon", None), P(), P(), P("lat", "lon", None))
    out_specs = (P("lat", "lon", None), P(), P())
    step = functools.partial(body, mesh.shape["lat"], mesh.shape["lon"])
    return jax.shard_map(step, mesh=mesh, in_specs=in_specs, out_specs=out_specs, check_vma=False)
```

time: 368 us -> 109 us (0.30)
  waiting for transfers between devices: 282 us -> 0 us
  Pallas kernels: 0 us -> 102 us
  starting transfers between devices: 30.4 us -> 0 us
  matrix products: 22.2 us -> 0 us
  between operations: 14.6 us -> 0.66 us
  local copies, waits for them, and re-layouts: 13.6 us -> 5.67 us
  other arithmetic: 4.03 us -> 0 us
    psum x1 -> x0, waiting for transfers between devices: 260 us -> none  [body(): lax.psum((first_part, second_part), ('lat', 'lon'))]
    pallas_call x0 -> x2, Pallas kernels: none -> 102 us  [the longest x1 55.2 us: body(): pl.pallas_call(functools.partial(reduce_kernel, ch, half), out_shape=(jax...]
    ppermute x16 -> x0, starting transfers between devices: 30.4 us -> none  [the longest x8 21.5 us: extended(): lax.ppermute(lax.slice_in_dim(block, 0, width, axis=dim), axis, backward)]
    dot_general x54 -> x0, matrix products: 22.2 us -> none  [the longest x18 8.1 us: conv_taps(): lax.dot_general(piece, weight[2 - first, 2 - second], (((1,), (1,)), ((),...]
    ppermute x16 -> x0, waiting for transfers between devices: 21.2 us -> none  [the longest x8 13.6 us: extended(): lax.ppermute(lax.slice_in_dim(block, block.shape[dim] - width, None, axis...]
    slice x9 -> x0, local copies, waits for them, and re-layouts: 4.87 us -> none  [the longest x4 3.98 us: conv_taps(): padded[first:first + rows, second:second + cols, :].reshape(rows * cols, -1)]
    unnamed x16 -> x7, local copies, waits for them, and re-layouts: 8.77 us -> 5.67 us
  transfers between devices with their start and end apart: 17 -> 0, of which waited for: 12 -> 0; matrix products, arithmetic and copies ran while one was open for 4% -> 0% of each run, Pallas kernels for 0% -> 0%
where the time goes in v1:
time: 109 us
  Pallas kernels  102 us (94%)
  local copies, waits for them, and re-layouts  5.67 us (5%)
    pallas_call x1, Pallas kernels, body(): pl.pallas_call(functools.partial(reduce_kernel, ch, half), out_shape=(jax...  55.2 us
    pallas_call x1, Pallas kernels, body(): pl.pallas_call(functools.partial(stage_kernel, lats, lons, rows, cols, ch...  47.2 us
    unnamed x7, local copies, waits for them, and re-layouts  5.67 us

profile of v1, /device:TPU:1, one launch (start us, length us, event | category | flops | bytes accessed | tf_op | source)
XLA Modules:
  0.0 108.7 jit_solution(6812737749090060360)
XLA Ops:
  0.6 47.2 %stages.1 = (bf16[16,96,256]{2,1,0:T(8,128)(2,1)}, f32[3,256,768]{2,1,0:T(8,128)}, f32[3,256,768]{2,1,0:T(8,128)}) custom-call(bf16[16,96,256]{2,1,0:T(8,128)(2,1)} %in_ref.1, bf16[3,768,256]{2,1,0:T(8,128)(2,1)} %bitcast.6, bf16[3,768,256]{2,1,0:T(8,128)(2,1)} %bitcast.7, bf16[16,96,256]{2,1,0:T(8,128)(2,1)} %cot_ref.1), custom_call_target="tpu_custom_call" | custom-call | tf_op jit(solution)/shard_map/stages/pallas_call | solution.py:405
  47.8 0.0 copy-start.1
  47.8 55.2 %reduce.1 = (f32[9,256,256]{2,1,0:T(8,128)}, f32[9,256,256]{2,1,0:T(8,128)}) custom-call(f32[3,256,768]{2,1,0:T(8,128)} %get-tuple-element.9.g1_ref, f32[3,256,768]{2,1,0:T(8,128)} %get-tuple-element.10.g2_ref), custom_call_target="tpu_custom_call" | custom-call | tf_op jit(solution)/shard_map/reduce/pallas_call | solution.py:437
  103.0 0.0 copy-done.1
  103.0 0.9 copy.10
  103.9 0.0 copy-start
  103.9 3.4 %copy.11 = f32[3,3,256,256]{3,2,1,0:T(8,128)} copy(f32[3,3,256,256]{3,2,1,0:T(8,128)} %bitcast.5) | data formatting | bytes 4718592
  107.3 0.0 copy-done
  107.3 1.4 %copy.12 = f32[3,3,256,256]{3,2,1,0:T(8,128)} copy(f32[3,3,256,256]{3,2,1,0:T(8,128)S(1)} %bitcast.4) | data formatting | bytes 4718592
Async XLA Ops:
  47.8 55.2 %copy-start.1 = (bf16[16,96,256]{2,1,0:T(8,128)(2,1)S(1)}, bf16[16,96,256]{2,1,0:T(8,128)(2,1)}, u32[]{:S(2)}) copy-start(bf16[16,96,256]{2,1,0:T(8,128)(2,1)} %get-tuple-element.16) | copy-start | bytes 2359300
  103.9 3.4 %copy-start = (f32[9,256,256]{2,1,0:T(8,128)S(1)}, f32[9,256,256]{2,1,0:T(8,128)}, u32[]{:S(2)}) copy-start(f32[9,256,256]{2,1,0:T(8,128)} %get-tuple-element.12) | copy-start | bytes 7077892

commit v2 on v0

v2 whole, which is shorter than its diff:
```python
import functools

import jax
import jax.numpy as jnp
from jax import lax
from jax.experimental import pallas as pl
from jax.experimental.pallas import tpu as pltpu
from jax.sharding import PartitionSpec as P

MESH = pl.DeviceIdType.MESH
F32 = jnp.float32
BF16 = jnp.bfloat16
VMEM_LIMIT = 56 * 1024 * 1024


def slope_parts(value):
    half = 0.5 * (1.0 + lax.erf(value * 0.7071067811865476))
    slope = half + value * jnp.exp(-0.5 * value * value) * 0.3989422804014327
    return half, slope


def kernel(
    lats, lons, rows, cols, ch, group,
    in_hbm, w1_hbm, w2_hbm, cot_hbm,
    dx_ref, o1_ref, o2_ref,
    in_ref, w1_ref, w2_ref, cot_ref,
    xs, acts, d2s, d1s, slope1, turned, edge, sent, got, halo,
    grads, pair, mine, out1, in1, zin, final,
    load_sem, send_sem, recv_sem,
    pair_sem, plane_sem, z_sem, spread_sem, last_sem,
):
    lat, lon = lax.axis_index("lat"), lax.axis_index("lon")
    core = lax.rem(lat, 2)
    x = lax.rem(lat // 2, 2) * 2 + lon // 8
    y = lat // 4
    z = lax.rem(lon, 8)
    size = group * cols
    blocks = rows // group
    half = ch // 2
    mid = slice(ch, 2 * ch)

    loads = [
        pltpu.make_async_copy(src, dst, load_sem.at[n])
        for n, (src, dst) in enumerate(
            ((in_hbm, in_ref), (w1_hbm, w1_ref), (cot_hbm, cot_ref), (w2_hbm, w2_ref))
        )
    ]
    for copy in loads:
        copy.start()

    def spot(dlat, dlon):
        return {"lat": lax.rem(lat + dlat + lats, lats), "lon": lax.rem(lon + dlon + lons, lons)}

    def at(x, y, z, core):
        return {"lat": y * 4 + (x // 2) * 2 + core, "lon": lax.rem(x, 2) * 8 + z}

    partner = at(x, y, z, 1 - core)
    plane = [(dx, dy) for dx in range(4) for dy in range(4) if dx or dy]

    def in_plane(dx, dy):
        return lax.rem(x + dx, 4), lax.rem(y + dy, 4)

    around = [(dlat, dlon) for dlat in (-1, 0, 1) for dlon in (-1, 0, 1) if dlat or dlon]
    peers = [spot(*shift) for shift in around] + [partner]
    peers += [at(*in_plane(*shift), z, core) for shift in plane]
    peers += [at(x, y, lax.rem(z + d, 8), core) for d in range(1, 8)]
    barrier = pltpu.get_barrier_semaphore()
    for peer in peers:
        pl.semaphore_signal(barrier, inc=1, device_id=peer, device_id_type=MESH)

    def remote(src, dst, sems, device):
        return pltpu.make_async_remote_copy(
            src_ref=src, dst_ref=dst, send_sem=sems.at[0], recv_sem=sems.at[1],
            device_id=device, device_id_type=MESH,
        )

    def put_row(field, row, value, mark=True):
        where = pl.ds(pl.multiple_of(row * cols, cols), cols)
        field[where, mid] = value.astype(BF16)
        field[where, 0:ch] = pltpu.roll(value, 1, 0).astype(BF16)
        field[where, 2 * ch : 3 * ch] = pltpu.roll(value, cols - 1, 0).astype(BF16)
        if mark:
            edge[0, pl.ds(row - 1, 1), :] = value[0:1]
            edge[1, pl.ds(row - 1, 1), :] = value[cols - 1 : cols]

    def copies(index, field, which):
        if index == 0:
            first, last = in_ref.at[0], in_ref.at[rows - 1]
        else:
            first = field.at[cols : 2 * cols, mid]
            last = field.at[rows * cols : (rows + 1) * cols, mid]
        plan = [
            (first, field.at[(rows + 1) * cols : (rows + 2) * cols, mid], (-1, 0)),
            (last, field.at[0:cols, mid], (1, 0)),
        ]
        for dlat in (-1, 1, 0):
            plan.append((sent.at[index, 0], got.at[index, 1, 1 - dlat], (dlat, -1)))
            plan.append((sent.at[index, 1], got.at[index, 0, 1 - dlat], (dlat, 1)))
        return [
            pltpu.make_async_remote_copy(
                src_ref=plan[n][0], dst_ref=plan[n][1],
                send_sem=send_sem.at[index, n], recv_sem=recv_sem.at[index, n],
                device_id=spot(*plan[n][2]), device_id_type=MESH,
            )
            for n in which
        ]

    def send(index, field):
        for side in range(2):
            sent[index, side] = edge[side].astype(BF16)
        for copy in copies(index, field, range(8)):
            copy.start()

    up, down = lat > 0, lat < lats - 1

    def receive_sides(index, field):
        for copy in copies(index, field, (6, 7)):
            copy.wait()
        for side in range(2):
            halo[side, 8 : 8 + rows] = got[index, side, 1].astype(F32)
        spots = lax.broadcasted_iota(jnp.int32, (16, ch), 0)
        for row in range(1, rows + 1):
            head = slice(row * cols, row * cols + 16)
            tail = slice((row + 1) * cols - 16, (row + 1) * cols)
            left = halo[0, 7 + row : 8 + row, :]
            right = halo[1, 7 + row : 8 + row, :]
            field[head, 0:ch] = jnp.where(spots == 0, left, field[head, 0:ch].astype(F32)).astype(BF16)
            field[tail, 2 * ch : 3 * ch] = jnp.where(
                spots == 15, right, field[tail, 2 * ch : 3 * ch].astype(F32)
            ).astype(BF16)

    def receive_ends(index, field):
        for copy in copies(index, field, range(6)):
            copy.wait()
        place = lax.broadcasted_iota(jnp.int32, (cols, ch), 0)
        for row, valid, slot, pick in ((0, up, 0, rows - 1), (rows + 1, down, 2, 0)):
            where = slice(row * cols, (row + 1) * cols)
            value = jnp.where(valid, field[where, mid].astype(F32), 0.0)
            left, right = (
                jnp.where(valid, got[index, side, slot].astype(F32)[pick : pick + 1], 0.0)
                for side in range(2)
            )
            field[where, mid] = value.astype(BF16)
            field[where, 0:ch] = jnp.where(place == 0, left, pltpu.roll(value, 1, 0)).astype(BF16)
            field[where, 2 * ch : 3 * ch] = jnp.where(
                place == cols - 1, right, pltpu.roll(value, cols - 1, 0)
            ).astype(BF16)

    def conv(field, weight, block):
        total = None
        for a in range(3):
            piece = field[pl.ds(pl.multiple_of((block * group + a) * cols, cols), size), :]
            part = jnp.dot(piece, weight[a], preferred_element_type=F32)
            total = part if total is None else total + part
        return total

    def conv_t(field, weight, block):
        total = None
        for a in range(3):
            for b in range(3):
                piece = field[
                    pl.ds(pl.multiple_of((block * group + a) * cols, cols), size), b * ch : (b + 1) * ch
                ]
                part = lax.dot_general(
                    piece, weight[2 - a, (2 - b) * ch : (3 - b) * ch, :],
                    (((1,), (1,)), ((), ())), preferred_element_type=F32,
                )
                total = part if total is None else total + part
        return total

    def put_block(field, block, value):
        for k in range(group):
            put_row(field, block * group + 1 + k, value[k * cols : (k + 1) * cols])

    def stage(index, field, step):
        receive_sides(index, field)
        lax.fori_loop(1, blocks - 1, step, 0)
        receive_ends(index, field)
        lax.fori_loop(0, 2, lambda i, carry: step(i * (blocks - 1), carry), 0)

    own_rows = pl.ds(pl.multiple_of(core * half, half), half)
    other_rows = pl.ds(pl.multiple_of((1 - core) * half, half), half)

    def chunk(px, py):
        return pl.ds(pl.multiple_of((px * 4 + py) * 16, 16), 16)

    my_chunk = chunk(x, y)

    def taps(a):
        return slice(3 * a, 3 * a + 3)

    def pair_copy(g, a):
        return remote(grads.at[g, a, other_rows, :], pair.at[g, a], pair_sem.at[g, a], partner)

    def settle(ref, sems):
        pltpu.make_async_copy(ref, ref, sems.at[0]).wait()
        pltpu.make_async_copy(ref, ref, sems.at[1]).wait()

    def grad_piece(g, a, field):
        grads[g, a] = jnp.dot(
            turned[...], field[a * cols : (a + rows) * cols, :], preferred_element_type=F32
        )
        pair_copy(g, a).start()

    def scatter(g, a):
        pair_copy(g, a).wait()
        for b in range(3):
            lanes = slice(b * ch, (b + 1) * ch)
            total = (grads[g, a, own_rows, lanes] + pair[g, a, :, lanes]).T
            mine[g, a * 3 + b] = total
            out1[g, a * 3 + b] = total.astype(BF16)
        for n, shift in enumerate(plane):
            px, py = in_plane(*shift)
            remote(
                out1.at[g, taps(a), chunk(px, py), :], in1.at[g, a, n],
                plane_sem.at[g, a], at(px, py, z, core),
            ).start()

    def depth(g, a):
        settle(in1.at[g, a], plane_sem.at[g, a])
        total = mine[g, taps(a), my_chunk, :]
        for n in range(15):
            total = total + in1[g, a, n].astype(F32)
        zin[g, a, z] = total.astype(BF16)
        for d in range(1, 8):
            remote(
                zin.at[g, a, z], zin.at[g, a, z], z_sem.at[g, a],
                at(x, y, lax.rem(z + d, 8), core),
            ).start()

    def spread(g, a):
        settle(zin.at[g, a, 0:7], z_sem.at[g, a])
        total = zin[g, a, 0].astype(F32)
        for n in range(1, 8):
            total = total + zin[g, a, n].astype(F32)
        final[g, core, taps(a), my_chunk, :] = total.astype(BF16)
        place = final.at[g, core, taps(a), my_chunk, :]
        for shift in plane:
            px, py = in_plane(*shift)
            remote(place, place, spread_sem.at[g, a], at(px, py, z, core)).start()

    def last_copy(g, a):
        place = final.at[g, core, taps(a)]
        return remote(place, place, last_sem.at[g, a], partner)

    def join(g, a):
        settle(in1.at[g, a], spread_sem.at[g, a])
        last_copy(g, a).start()

    def finish(g, a):
        last_copy(g, a).wait()
        out = (o2_ref, o1_ref)[g]
        for c in range(2):
            out[taps(a), :, c * half : (c + 1) * half] = final[g, c, taps(a)]

    loads[0].wait()
    for row in range(rows):
        edge[0, row : row + 1] = in_ref[row, 0:16].astype(F32)[0:1]
        edge[1, row : row + 1] = in_ref[row, cols - 16 : cols].astype(F32)[15:16]
    pl.semaphore_wait(barrier, len(peers))
    send(0, xs)

    def load(row, carry):
        put_row(xs, row + 1, in_ref[row].astype(F32), mark=False)
        return carry

    lax.fori_loop(0, rows, load, 0)
    loads[1].wait()

    def first(block, carry):
        value = conv(xs, w1_ref, block)
        part, slope = slope_parts(value)
        slope1[pl.ds(pl.multiple_of(block * size, size), size), :] = slope
        put_block(acts, block, value * part)
        return carry

    stage(0, xs, first)
    send(1, acts)
    loads[2].wait()
    loads[3].wait()

    def second(block, carry):
        value = conv(acts, w2_ref, block)
        _, slope = slope_parts(value)
        rate = cot_ref[pl.ds(block * group, group)].astype(F32).reshape(size, ch)
        delta = rate * slope
        put_block(d2s, block, delta)
        turned[:, pl.ds(pl.multiple_of(block * size, size), size)] = delta.T.astype(BF16)
        return carry

    stage(1, acts, second)
    send(2, d2s)
    grad_piece(0, 0, acts)
    grad_piece(0, 1, acts)
    scatter(0, 0)
    grad_piece(0, 2, acts)
    scatter(0, 1)
    scatter(0, 2)

    def third(block, carry):
        value = conv_t(d2s, w2_ref, block)
        delta = value * slope1[pl.ds(pl.multiple_of(block * size, size), size), :]
        put_block(d1s, block, delta)
        turned[:, pl.ds(pl.multiple_of(block * size, size), size)] = delta.T.astype(BF16)
        return carry

    stage(2, d2s, third)
    send(3, d1s)
    grad_piece(1, 0, xs)
    grad_piece(1, 1, xs)
    scatter(1, 0)
    grad_piece(1, 2, xs)
    scatter(1, 1)
    scatter(1, 2)
    depth(0, 0)
    depth(0, 1)

    def fourth(block, carry):
        value = conv_t(d1s, w1_ref, block)
        dx_ref[pl.ds(block * group, group)] = value.astype(BF16).reshape(group, cols, ch)
        return carry

    receive_sides(3, d1s)
    lax.fori_loop(1, blocks - 1, fourth, 0)
    depth(0, 2)
    receive_ends(3, d1s)
    lax.fori_loop(0, 2, lambda i, carry: fourth(i * (blocks - 1), carry), 0)
    depth(1, 0)
    spread(0, 0)
    depth(1, 1)
    spread(0, 1)
    depth(1, 2)
    spread(0, 2)
    spread(1, 0)
    join(0, 0)
    spread(1, 1)
    join(0, 1)
    spread(1, 2)
    join(0, 2)
    finish(0, 0)
    finish(0, 1)
    finish(0, 2)
    join(1, 0)
    join(1, 1)
    finish(1, 0)
    join(1, 2)
    finish(1, 1)
    finish(1, 2)


def body(lats, lons, inputs, first_filter, second_filter, cotangent):
    rows, cols, ch = inputs.shape
    group = 4
    vmem = pl.BlockSpec(memory_space=pltpu.VMEM)
    hbm = pl.BlockSpec(memory_space=pl.ANY)
    cells = rows * cols
    half = ch // 2
    padded = pltpu.VMEM(((rows + 2) * cols, 3 * ch), BF16)
    dma = pltpu.SemaphoreType.DMA
    dx, o1, o2 = pl.pallas_call(
        functools.partial(kernel, lats, lons, rows, cols, ch, group),
        out_shape=(
            jax.ShapeDtypeStruct((rows, cols, ch), BF16),
            jax.ShapeDtypeStruct((9, ch, ch), BF16),
            jax.ShapeDtypeStruct((9, ch, ch), BF16),
        ),
        in_specs=[hbm] * 4,
        out_specs=(vmem,) * 3,
        scratch_shapes=[
            pltpu.VMEM((rows, cols, ch), BF16),
            pltpu.VMEM((3, 3 * ch, ch), BF16),
            pltpu.VMEM((3, 3 * ch, ch), BF16),
            pltpu.VMEM((rows, cols, ch), BF16),
            padded, padded, padded, padded,
            pltpu.VMEM((cells, ch), F32),
            pltpu.VMEM((ch, cells), BF16),
            pltpu.VMEM((2, rows, ch), F32),
            pltpu.VMEM((4, 2, rows, ch), BF16),
            pltpu.VMEM((4, 2, 3, rows, ch), BF16),
            pltpu.VMEM((2, 16 + rows, ch), F32),
            pltpu.VMEM((2, 3, ch, 3 * ch), F32),
            pltpu.VMEM((2, 3, half, 3 * ch), F32),
            pltpu.VMEM((2, 9, ch, half), F32),
            pltpu.VMEM((2, 9, ch, half), BF16),
            pltpu.VMEM((2, 3, 15, 3, 16, half), BF16),
            pltpu.VMEM((2, 3, 8, 3, 16, half), BF16),
            pltpu.VMEM((2, 2, 9, ch, half), BF16),
            dma((4,)), dma((4, 8)), dma((4, 8)),
            dma((2, 3, 2)), dma((2, 3, 2)), dma((2, 3, 2)), dma((2, 3, 2)), dma((2, 3, 2)),
        ],
        compiler_params=pltpu.CompilerParams(
            collective_id=0, has_side_effects=True, vmem_limit_bytes=VMEM_LIMIT
        ),
        name="stages",
    )(
        inputs,
        first_filter.reshape(3, 3 * ch, ch),
        second_filter.reshape(3, 3 * ch, ch),
        cotangent,
    )
    return dx, o1.astype(F32).reshape(3, 3, ch, ch), o2.astype(F32).reshape(3, 3, ch, ch)


def solution(mesh):
    in_specs = (P("lat", "lon", None), P(), P(), P("lat", "lon", None))
    out_specs = (P("lat", "lon", None), P(), P())
    step = functools.partial(body, mesh.shape["lat"], mesh.shape["lon"])
    return jax.shard_map(step, mesh=mesh, in_specs=in_specs, out_specs=out_specs, check_vma=False)
```

time: 368 us -> 71.1 us (0.19)
  waiting for transfers between devices: 282 us -> 0 us
  Pallas kernels: 0 us -> 64.9 us
  starting transfers between devices: 30.4 us -> 0 us
  matrix products: 22.2 us -> 0 us
  between operations: 14.6 us -> 0.65 us
  local copies, waits for them, and re-layouts: 13.6 us -> 0.89 us
    psum x1 -> x0, waiting for transfers between devices: 260 us -> none  [body(): lax.psum((first_part, second_part), ('lat', 'lon'))]
    pallas_call x0 -> x1, Pallas kernels: none -> 64.9 us  [body(): pl.pallas_call(functools.partial(kernel, lats, lons, rows, cols, ch, grou...]
    ppermute x16 -> x0, starting transfers between devices: 30.4 us -> none  [the longest x8 21.5 us: extended(): lax.ppermute(lax.slice_in_dim(block, 0, width, axis=dim), axis, backward)]
    dot_general x54 -> x0, matrix products: 22.2 us -> none  [the longest x18 8.1 us: conv_taps(): lax.dot_general(piece, weight[2 - first, 2 - second], (((1,), (1,)), ((),...]
    ppermute x16 -> x0, waiting for transfers between devices: 21.2 us -> none  [the longest x8 13.6 us: extended(): lax.ppermute(lax.slice_in_dim(block, block.shape[dim] - width, None, axis...]
    unnamed x16 -> x5, local copies, waits for them, and re-layouts: 8.77 us -> 0.89 us
    slice x9 -> x0, local copies, waits for them, and re-layouts: 4.87 us -> none  [the longest x4 3.98 us: conv_taps(): padded[first:first + rows, second:second + cols, :].reshape(rows * cols, -1)]
    reshape x0 -> x2, other arithmetic: none -> 4.62 us  [the longest x1 2.99 us: body(): o1.astype(F32).reshape(3, 3, ch, ch)]
  transfers between devices with their start and end apart: 17 -> 0, of which waited for: 12 -> 0; matrix products, arithmetic and copies ran while one was open for 4% -> 0% of each run, Pallas kernels for 0% -> 0%
where the time goes in v2:
time: 71.1 us; the launch traced here: 71 us
  Pallas kernels  64.9 us (91%)
  other arithmetic  4.62 us (6%)
  local copies, waits for them, and re-layouts  0.89 us (1%)
    pallas_call x1, Pallas kernels, body(): pl.pallas_call(functools.partial(kernel, lats, lons, rows, cols, ch, grou...  64.9 us
    reshape x1, other arithmetic, body(): o1.astype(F32).reshape(3, 3, ch, ch)  2.99 us
    reshape x1, other arithmetic, body(): o2.astype(F32).reshape(3, 3, ch, ch)  1.63 us

profile of v2, /device:TPU:1, one launch (start us, length us, event | category | flops | bytes accessed | tf_op | source)
XLA Modules:
  0.0 71.0 jit_solution(11361372416641789925)
XLA Ops:
  0.6 64.9 %stages.1 = (bf16[16,96,256]{2,1,0:T(8,128)(2,1)}, bf16[9,256,256]{2,1,0:T(8,128)(2,1)}, bf16[9,256,256]{2,1,0:T(8,128)(2,1)}) custom-call(bf16[16,96,256]{2,1,0:T(8,128)(2,1)} %in_hbm.1, bf16[3,768,256]{2,1,0:T(8,128)(2,1)} %bitcast.8, bf16[3,768,256]{2,1,0:T(8,128)(2,1)} %bitcast.9, bf16[16,96,256]{2,1,0:T(8,128)(2,1)} %cot_hbm.1), custom_call_target="tpu_custom_call" | custom-call | tf_op jit(solution)/shard_map/stages/pallas_call | solution.py:360
  65.5 0.0 copy-start
  65.5 3.0 %convert.2 = f32[3,3,256,256]{3,2,1,0:T(8,128)} convert(bf16[3,3,256,256]{3,2,1,0:T(8,128)(2,1)} %bitcast.7) | non-fusion elementwise | flops 589824 | bytes 3538944 | tf_op jit(solution)/shard_map/reshape | solution.py:401
  68.5 0.0 copy-done
  68.5 0.0 copy-start.1
  68.5 1.6 %convert.3 = f32[3,3,256,256]{3,2,1,0:T(8,128)} convert(bf16[3,3,256,256]{3,2,1,0:T(8,128)(2,1)S(1)} %bitcast.6) | non-fusion elementwise | flops 589824 | bytes 3538944 | tf_op jit(solution)/shard_map/reshape | solution.py:401
  70.2 0.0 copy-done.1
  70.2 0.9 %copy.8 = bf16[16,96,256]{2,1,0:T(8,128)(2,1)} copy(bf16[16,96,256]{2,1,0:T(8,128)(2,1)S(1)} %copy-done.1) | data formatting | bytes 1572864
Async XLA Ops:
  65.5 3.0 %copy-start = (bf16[9,256,256]{2,1,0:T(8,128)(2,1)S(1)}, bf16[9,256,256]{2,1,0:T(8,128)(2,1)}, u32[]{:S(2)}) copy-start(bf16[9,256,256]{2,1,0:T(8,128)(2,1)} %get-tuple-element.8) | copy-start | bytes 3538948
  68.5 1.6 %copy-start.1 = (bf16[16,96,256]{2,1,0:T(8,128)(2,1)S(1)}, bf16[16,96,256]{2,1,0:T(8,128)(2,1)}, u32[]{:S(2)}) copy-start(bf16[16,96,256]{2,1,0:T(8,128)(2,1)} %get-tuple-element.12) | copy-start | bytes 2359300

commit v3 on v2

--- a/solution.py
+++ b/solution.py
@@ -10,7 +10,8 @@
 MESH = pl.DeviceIdType.MESH
 F32 = jnp.float32
 BF16 = jnp.bfloat16
-VMEM_LIMIT = 56 * 1024 * 1024
+VMEM_LIMIT = 44 * 1024 * 1024
+MID = 4
 
 
 def slope_parts(value):
@@ -35,7 +36,6 @@
     y = lat // 4
     z = lax.rem(lon, 8)
     size = group * cols
-    blocks = rows // group
     half = ch // 2
     mid = slice(ch, 2 * ch)
 
@@ -75,7 +75,7 @@
         )
 
     def put_row(field, row, value, mark=True):
-        where = pl.ds(pl.multiple_of(row * cols, cols), cols)
+        where = pl.ds(row * cols if isinstance(row, int) else pl.multiple_of(row * cols, cols), cols)
         field[where, mid] = value.astype(BF16)
         field[where, 0:ch] = pltpu.roll(value, 1, 0).astype(BF16)
         field[where, 2 * ch : 3 * ch] = pltpu.roll(value, cols - 1, 0).astype(BF16)
@@ -146,21 +146,19 @@
                 place == cols - 1, right, pltpu.roll(value, cols - 1, 0)
             ).astype(BF16)
 
-    def conv(field, weight, block):
+    def conv(field, weight, start, count):
         total = None
         for a in range(3):
-            piece = field[pl.ds(pl.multiple_of((block * group + a) * cols, cols), size), :]
+            piece = field[(start + a) * cols : (start + a + count) * cols, :]
             part = jnp.dot(piece, weight[a], preferred_element_type=F32)
             total = part if total is None else total + part
         return total
 
-    def conv_t(field, weight, block):
+    def conv_t(field, weight, start, count):
         total = None
         for a in range(3):
             for b in range(3):
-                piece = field[
-                    pl.ds(pl.multiple_of((block * group + a) * cols, cols), size), b * ch : (b + 1) * ch
-                ]
+                piece = field[(start + a) * cols : (start + a + count) * cols, b * ch : (b + 1) * ch]
                 part = lax.dot_general(
                     piece, weight[2 - a, (2 - b) * ch : (3 - b) * ch, :],
                     (((1,), (1,)), ((), ())), preferred_element_type=F32,
@@ -168,15 +166,17 @@
                 total = part if total is None else total + part
         return total
 
-    def put_block(field, block, value):
-        for k in range(group):
-            put_row(field, block * group + 1 + k, value[k * cols : (k + 1) * cols])
-
-    def stage(index, field, step):
-        receive_sides(index, field)
-        lax.fori_loop(1, blocks - 1, step, 0)
-        receive_ends(index, field)
-        lax.fori_loop(0, 2, lambda i, carry: step(i * (blocks - 1), carry), 0)
+    def put_rows(field, start, count, value):
+        for k in range(count):
+            put_row(field, start + 1 + k, value[k * cols : (k + 1) * cols])
+
+    def middle(step):
+        for start in range(group, rows - group, MID):
+            step(start, MID)
+
+    def outer(step):
+        step(0, group)
+        step(rows - group, group)
 
     own_rows = pl.ds(pl.multiple_of(core * half, half), half)
     other_rows = pl.ds(pl.multiple_of((1 - core) * half, half), half)
@@ -186,11 +186,22 @@
 
     my_chunk = chunk(x, y)
 
-    def taps(a):
-        return slice(3 * a, 3 * a + 3)
-
-    def pair_copy(g, a):
-        return remote(grads.at[g, a, other_rows, :], pair.at[g, a], pair_sem.at[g, a], partner)
+    pieces = [(0, 3 * a, 3) for a in range(3)] + [(1, t, 1) for t in range(9)]
+    number = {piece: n for n, piece in enumerate(pieces)}
+
+    def taps(piece):
+        return slice(piece[1], piece[1] + piece[2])
+
+    def lanes(piece):
+        first = piece[1] % 3
+        return slice(first * ch, (first + piece[2]) * ch)
+
+    def pair_copy(piece):
+        g, t, _ = piece
+        return remote(
+            grads.at[g, t // 3, other_rows, lanes(piece)], pair.at[g, t // 3, :, lanes(piece)],
+            pair_sem.at[number[piece]], partner,
+        )
 
     def settle(ref, sems):
         pltpu.make_async_copy(ref, ref, sems.at[0]).wait()
@@ -200,58 +211,68 @@
         grads[g, a] = jnp.dot(
             turned[...], field[a * cols : (a + rows) * cols, :], preferred_element_type=F32
         )
-        pair_copy(g, a).start()
-
-    def scatter(g, a):
-        pair_copy(g, a).wait()
-        for b in range(3):
-            lanes = slice(b * ch, (b + 1) * ch)
-            total = (grads[g, a, own_rows, lanes] + pair[g, a, :, lanes]).T
-            mine[g, a * 3 + b] = total
-            out1[g, a * 3 + b] = total.astype(BF16)
+        for piece in pieces:
+            if piece[0] == g and piece[1] // 3 == a:
+                pair_copy(piece).start()
+
+    def scatter(piece):
+        g, first, count = piece
+        pair_copy(piece).wait()
+        for t in range(first, first + count):
+            a, b = t // 3, t % 3
+            where = slice(b * ch, (b + 1) * ch)
+            total = (grads[g, a, own_rows, where] + pair[g, a, :, where]).T
+            mine[g, t] = total
+            out1[g, t] = total.astype(BF16)
         for n, shift in enumerate(plane):
             px, py = in_plane(*shift)
             remote(
-                out1.at[g, taps(a), chunk(px, py), :], in1.at[g, a, n],
-                plane_sem.at[g, a], at(px, py, z, core),
+                out1.at[g, taps(piece), chunk(px, py), :], in1.at[g, taps(piece), n],
+                plane_sem.at[number[piece]], at(px, py, z, core),
             ).start()
 
-    def depth(g, a):
-        settle(in1.at[g, a], plane_sem.at[g, a])
-        total = mine[g, taps(a), my_chunk, :]
+    def depth(piece):
+        g = piece[0]
+        settle(in1.at[g, taps(piece)], plane_sem.at[number[piece]])
+        total = mine[g, taps(piece), my_chunk, :]
         for n in range(15):
-            total = total + in1[g, a, n].astype(F32)
-        zin[g, a, z] = total.astype(BF16)
+            total = total + in1[g, taps(piece), n].astype(F32)
+        zin[g, taps(piece), z] = total.astype(BF16)
         for d in range(1, 8):
-            remote(
-                zin.at[g, a, z], zin.at[g, a, z], z_sem.at[g, a],
-                at(x, y, lax.rem(z + d, 8), core),
-            ).start()
-
-    def spread(g, a):
-        settle(zin.at[g, a, 0:7], z_sem.at[g, a])
-        total = zin[g, a, 0].astype(F32)
+            place = zin.at[g, taps(piece), z]
+            remote(place, place, z_sem.at[number[piece]], at(x, y, lax.rem(z + d, 8), core)).start()
+
+    def spread(piece):
+        g = piece[0]
+        settle(zin.at[g, taps(piece), 0:7], z_sem.at[number[piece]])
+        total = zin[g, taps(piece), 0].astype(F32)
         for n in range(1, 8):
-            total = total + zin[g, a, n].astype(F32)
-        final[g, core, taps(a), my_chunk, :] = total.astype(BF16)
-        place = final.at[g, core, taps(a), my_chunk, :]
+            total = total + zin[g, taps(piece), n].astype(F32)
+        final[g, core, taps(piece), my_chunk, :] = total.astype(BF16)
+        place = final.at[g, core, taps(piece), my_chunk, :]
         for shift in plane:
             px, py = in_plane(*shift)
-            remote(place, place, spread_sem.at[g, a], at(px, py, z, core)).start()
-
-    def last_copy(g, a):
-        place = final.at[g, core, taps(a)]
-        return remote(place, place, last_sem.at[g, a], partner)
-
-    def join(g, a):
-        settle(in1.at[g, a], spread_sem.at[g, a])
-        last_copy(g, a).start()
-
-    def finish(g, a):
-        last_copy(g, a).wait()
-        out = (o2_ref, o1_ref)[g]
+            remote(place, place, spread_sem.at[number[piece]], at(px, py, z, core)).start()
+
+    def last_copy(piece):
+        place = final.at[piece[0], core, taps(piece)]
+        return remote(place, place, last_sem.at[number[piece]], partner)
+
+    def join(piece):
+        settle(in1.at[piece[0], taps(piece)], spread_sem.at[number[piece]])
+        last_copy(piece).start()
+
+    def finish(piece):
+        last_copy(piece).wait()
+        out = (o2_ref, o1_ref)[piece[0]]
         for c in range(2):
-            out[taps(a), :, c * half : (c + 1) * half] = final[g, c, taps(a)]
+            out[taps(piece), :, c * half : (c + 1) * half] = final[piece[0], c, taps(piece)]
+
+    early, late = pieces[:3], [pieces[3 + 3 * a : 6 + 3 * a] for a in range(3)]
+
+    def each(step, some):
+        for piece in some:
+            step(piece)
 
     loads[0].wait()
     for row in range(rows):
@@ -267,92 +288,107 @@
     lax.fori_loop(0, rows, load, 0)
     loads[1].wait()
 
-    def first(block, carry):
-        value = conv(xs, w1_ref, block)
+    def span(start, count):
+        return slice(start * cols, (start + count) * cols)
+
+    def first(start, count):
+        value = conv(xs, w1_ref, start, count)
         part, slope = slope_parts(value)
-        slope1[pl.ds(pl.multiple_of(block * size, size), size), :] = slope
-        put_block(acts, block, value * part)
-        return carry
-
-    stage(0, xs, first)
+        slope1[span(start, count), :] = slope
+        put_rows(acts, start, count, value * part)
+
+    receive_sides(0, xs)
+    middle(first)
+    receive_ends(0, xs)
+    outer(first)
     send(1, acts)
     loads[2].wait()
     loads[3].wait()
 
-    def second(block, carry):
-        value = conv(acts, w2_ref, block)
+    def second(start, count):
+        value = conv(acts, w2_ref, start, count)
         _, slope = slope_parts(value)
-        rate = cot_ref[pl.ds(block * group, group)].astype(F32).reshape(size, ch)
+        rate = cot_ref[start : start + count].astype(F32).reshape(count * cols, ch)
         delta = rate * slope
-        put_block(d2s, block, delta)
-        turned[:, pl.ds(pl.multiple_of(block * size, size), size)] = delta.T.astype(BF16)
-        return carry
-
-    stage(1, acts, second)
+        put_rows(d2s, start, count, delta)
+        turned[:, span(start, count)] = delta.T.astype(BF16)
+
+    receive_sides(1, acts)
+    middle(second)
+    receive_ends(1, acts)
+    outer(second)
     send(2, d2s)
     grad_piece(0, 0, acts)
     grad_piece(0, 1, acts)
-    scatter(0, 0)
+    scatter(early[0])
     grad_piece(0, 2, acts)
-    scatter(0, 1)
-    scatter(0, 2)
-
-    def third(block, carry):
-        value = conv_t(d2s, w2_ref, block)
-        delta = value * slope1[pl.ds(pl.multiple_of(block * size, size), size), :]
-        put_block(d1s, block, delta)
-        turned[:, pl.ds(pl.multiple_of(block * size, size), size)] = delta.T.astype(BF16)
-        return carry
-
-    stage(2, d2s, third)
+
+    def third(start, count):
+        value = conv_t(d2s, w2_ref, start, count)
+        delta = value * slope1[span(start, count), :]
+        put_rows(d1s, start, count, delta)
+        turned[:, span(start, count)] = delta.T.astype(BF16)
+
+    receive_sides(2, d2s)
+    middle(third)
+    each(scatter, early[1:])
+    receive_ends(2, d2s)
+    outer(third)
     send(3, d1s)
     grad_piece(1, 0, xs)
     grad_piece(1, 1, xs)
-    scatter(1, 0)
+    each(scatter, late[0])
+    depth(early[0])
     grad_piece(1, 2, xs)
-    scatter(1, 1)
-    scatter(1, 2)
-    depth(0, 0)
-    depth(0, 1)
-
-    def fourth(block, carry):
-        value = conv_t(d1s, w1_ref, block)
-        dx_ref[pl.ds(block * group, group)] = value.astype(BF16).reshape(group, cols, ch)
-        return carry
+    each(scatter, late[1])
+
+    def fourth(start, count):
+        value = conv_t(d1s, w1_ref, start, count)
+        dx_ref[start : start + count] = value.astype(BF16).reshape(count, cols, ch)
 
     receive_sides(3, d1s)
-    lax.fori_loop(1, blocks - 1, fourth, 0)
-    depth(0, 2)
+    middle(fourth)
+    each(scatter, late[2])
+    depth(early[1])
     receive_ends(3, d1s)
-    lax.fori_loop(0, 2, lambda i, carry: fourth(i * (blocks - 1), carry), 0)
-    depth(1, 0)
-    spread(0, 0)
-    depth(1, 1)
-    spread(0, 1)
-    depth(1, 2)
-    spread(0, 2)
-    spread(1, 0)
-    join(0, 0)
-    spread(1, 1)
-    join(0, 1)
-    spread(1, 2)
-    join(0, 2)
-    finish(0, 0)
-    finish(0, 1)
-    finish(0, 2)
-    join(1, 0)
-    join(1, 1)
-    finish(1, 0)
-    join(1, 2)
-    finish(1, 1)
-    finish(1, 2)
+    outer(fourth)
+    depth(early[2])
+    each(depth, late[0])
+    spread(early[0])
+    each(depth, late[1])
+    spread(early[1])
+    each(depth, late[2])
+    spread(early[2])
+    each(spread, late[0])
+    join(early[0])
+    each(spread, late[1])
+    join(early[1])
+    each(spread, late[2])
+    join(early[2])
+    each(finish, early)
+    for some in late:
+        each(join, some)
+    for some in late:
+        each(finish, some)
+
+
+def write_kernel(dx_ref, g1_ref, g2_ref, dx_out, o1_out, o2_out, wide, sems):
+    copies = [pltpu.make_async_copy(dx_ref, dx_out, sems.at[18])]
+    copies[0].start()
+    for n, (ref, out) in enumerate(((g1_ref, o1_out), (g2_ref, o2_out))):
+        for t in range(9):
+            wide[n, t] = ref[t].astype(F32)
+            copies.append(pltpu.make_async_copy(wide.at[n, t], out.at[t], sems.at[9 * n + t]))
+            copies[-1].start()
+    for copy in copies:
+        copy.wait()
 
 
 def body(lats, lons, inputs, first_filter, second_filter, cotangent):
     rows, cols, ch = inputs.shape
     group = 4
     vmem = pl.BlockSpec(memory_space=pltpu.VMEM)
-    hbm = pl.BlockSpec(memory_space=pl.ANY)
+    hbm = pl.BlockSpec(memory_space=pltpu.HBM)
     cells = rows * cols
     half = ch // 2
     padded = pltpu.VMEM(((rows + 2) * cols, 3 * ch), BF16)
@@ -382,23 +418,41 @@
             pltpu.VMEM((2, 3, half, 3 * ch), F32),
             pltpu.VMEM((2, 9, ch, half), F32),
             pltpu.VMEM((2, 9, ch, half), BF16),
-            pltpu.VMEM((2, 3, 15, 3, 16, half), BF16),
-            pltpu.VMEM((2, 3, 8, 3, 16, half), BF16),
+            pltpu.VMEM((2, 9, 15, 16, half), BF16),
+            pltpu.VMEM((2, 9, 8, 16, half), BF16),
             pltpu.VMEM((2, 2, 9, ch, half), BF16),
             dma((4,)), dma((4, 8)), dma((4, 8)),
-            dma((2, 3, 2)), dma((2, 3, 2)), dma((2, 3, 2)), dma((2, 3, 2)), dma((2, 3, 2)),
+            dma((12, 2)), dma((12, 2)), dma((12, 2)), dma((12, 2)), dma((12, 2)),
         ],
         compiler_params=pltpu.CompilerParams(
             collective_id=0, has_side_effects=True, vmem_limit_bytes=VMEM_LIMIT
         ),
         name="stages",
     )(
-        inputs,
-        first_filter.reshape(3, 3 * ch, ch),
-        second_filter.reshape(3, 3 * ch, ch),
-        cotangent,
+        *(
+            pltpu.with_memory_space_constraint(value, pltpu.HBM)
+            for value in (
+                inputs,
+                first_filter.reshape(3, 3 * ch, ch),
+                second_filter.reshape(3, 3 * ch, ch),
+                cotangent,
+            )
+        )
     )
-    return dx, o1.astype(F32).reshape(3, 3, ch, ch), o2.astype(F32).reshape(3, 3, ch, ch)
+    dx, o1, o2 = pl.pallas_call(
+        write_kernel,
+        out_shape=(
+            jax.ShapeDtypeStruct((rows, cols, ch), BF16),
+            jax.ShapeDtypeStruct((9, ch, ch), F32),
+            jax.ShapeDtypeStruct((9, ch, ch), F32),
+        ),
+        in_specs=[vmem] * 3,
+        out_specs=(hbm,) * 3,
+        scratch_shapes=[pltpu.VMEM((2, 9, ch, ch), F32), dma((19,))],
+        compiler_params=pltpu.CompilerParams(vmem_limit_bytes=12 * 1024 * 1024),
+        name="write",
+    )(dx, o1, o2)
+    return dx, o1.reshape(3, 3, ch, ch), o2.reshape(3, 3, ch, ch)
 
 
 def solution(mesh):

time: 71.1 us -> 65.8 us (0.925)
  other arithmetic: 4.62 us -> 0 us
  local copies, waits for them, and re-layouts: 0.89 us -> 0 us
    reshape x2 -> x0, other arithmetic: 4.62 us -> none  [the longest x1 2.99 us: body(): o1.astype(F32).reshape(3, 3, ch, ch)]
    pallas_call x0 -> x1, Pallas kernels: none -> 2.56 us  [body(): pl.pallas_call(write_kernel, out_shape=(jax.ShapeDtypeStruct((rows, cols,...]
    pallas_call x1, Pallas kernels: 64.9 us -> 62.3 us  [body(): pl.pallas_call(functools.partial(kernel, lats, lons, rows, cols, ch, grou...]
    unnamed x5 -> x0, local copies, waits for them, and re-layouts: 0.89 us -> none
where the time goes in v3:
time: 65.8 us; the launch traced here: 65.7 us
  Pallas kernels  64.9 us (99%)
  between operations  0.8 us (1%)
    pallas_call x1, Pallas kernels, body(): pl.pallas_call(functools.partial(kernel, lats, lons, rows, cols, ch, grou...  62.3 us
    pallas_call x1, Pallas kernels, body(): pl.pallas_call(write_kernel, out_shape=(jax.ShapeDtypeStruct((rows, cols,...  2.56 us

profile of v3, /device:TPU:1, one launch (start us, length us, event | category | flops | bytes accessed | tf_op | source)
XLA Modules:
  0.0 65.7 jit_solution(2467604554726443980)
XLA Ops:
  0.6 62.3 %stages.1 = (bf16[16,96,256]{2,1,0:T(8,128)(2,1)S(1)}, bf16[9,256,256]{2,1,0:T(8,128)(2,1)S(1)}, bf16[9,256,256]{2,1,0:T(8,128)(2,1)S(1)}) custom-call(bf16[16,96,256]{2,1,0:T(8,128)(2,1)} %in_hbm.1, bf16[3,768,256]{2,1,0:T(8,128)(2,1)} %bitcast.4, bf16[3,768,256]{2,1,0:T(8,128)(2,1)} %bitcast.5, bf16[16,96,256]{2,1,0:T(8,128)(2,1)} %cot_hbm.1), custom_call_target="tpu_custom_call" | custom-call | tf_op jit(solution)/shard_map/stages/pallas_call | solution.py:396
  63.0 2.6 %write.1 = (bf16[16,96,256]{2,1,0:T(8,128)(2,1)}, f32[9,256,256]{2,1,0:T(8,128)}, f32[9,256,256]{2,1,0:T(8,128)}) custom-call(bf16[16,96,256]{2,1,0:T(8,128)(2,1)S(1)} %get-tuple-element.9.dx_ref, bf16[9,256,256]{2,1,0:T(8,128)(2,1)S(1)} %get-tuple-element.10.g1_ref, bf16[9,256,256]{2,1,0:T(8,128)(2,1)S(1)} %get-tuple-element.11.g2_ref), custom_call_target="tpu_custom_call" | custom-call | tf_op jit(solution)/shard_map/write/pallas_call | solution.py:442

commit v4 on v3

--- a/solution.py
+++ b/solution.py
@@ -10,23 +10,25 @@
 MESH = pl.DeviceIdType.MESH
 F32 = jnp.float32
 BF16 = jnp.bfloat16
-VMEM_LIMIT = 44 * 1024 * 1024
-MID = 4
-
-
-def slope_parts(value):
-    half = 0.5 * (1.0 + lax.erf(value * 0.7071067811865476))
-    slope = half + value * jnp.exp(-0.5 * value * value) * 0.3989422804014327
-    return half, slope
+VMEM_LIMIT = 48 * 1024 * 1024
+B1, B2, B3, B4 = 4, 4, 4, 4
+
+
+def half_erf(value):
+    return 0.5 * (1.0 + lax.erf(value * 0.7071067811865476))
+
+
+def slope_of(value):
+    return half_erf(value) + value * jnp.exp(-0.5 * value * value) * 0.3989422804014327
 
 
 def kernel(
     lats, lons, rows, cols, ch, group,
     in_hbm, w1_hbm, w2_hbm, cot_hbm,
-    dx_ref, o1_ref, o2_ref,
-    in_ref, w1_ref, w2_ref, cot_ref,
-    xs, acts, d2s, d1s, slope1, turned, edge, sent, got, halo,
-    grads, pair, mine, out1, in1, zin, final,
+    dx_ref, final, o2_ref,
+    in_ref, w1_ref, w2_ref, cot_ref, wt1, wt2,
+    xs, acts, d2s, d1s, partial, slope1, turned, edge, sent, got, halo,
+    grads, pair, mine, out1, in1, zin,
     load_sem, send_sem, recv_sem,
     pair_sem, plane_sem, z_sem, spread_sem, last_sem,
 ):
@@ -74,14 +76,18 @@
             device_id=device, device_id_type=MESH,
         )
 
-    def put_row(field, row, value, mark=True):
-        where = pl.ds(row * cols if isinstance(row, int) else pl.multiple_of(row * cols, cols), cols)
-        field[where, mid] = value.astype(BF16)
-        field[where, 0:ch] = pltpu.roll(value, 1, 0).astype(BF16)
-        field[where, 2 * ch : 3 * ch] = pltpu.roll(value, cols - 1, 0).astype(BF16)
+    def line(row):
+        return pl.ds(row * cols if isinstance(row, int) else pl.multiple_of(row * cols, cols), cols)
+
+    def put_mid(field, row, value, mark=True):
+        field[line(row), mid] = value.astype(BF16)
         if mark:
-            edge[0, pl.ds(row - 1, 1), :] = value[0:1]
-            edge[1, pl.ds(row - 1, 1), :] = value[cols - 1 : cols]
+            edge[0, row - 1 : row] = value[0:1]
+            edge[1, row - 1 : row] = value[cols - 1 : cols]
+
+    def put_sides(field, row, value):
+        field[line(row), 0:ch] = pltpu.roll(value, 1, 0).astype(BF16)
+        field[line(row), 2 * ch : 3 * ch] = pltpu.roll(value, cols - 1, 0).astype(BF16)
 
     def copies(index, field, which):
         if index == 0:
@@ -154,29 +160,54 @@
             total = part if total is None else total + part
         return total
 
-    def conv_t(field, weight, start, count):
-        total = None
+    def flip(source, target):
         for a in range(3):
             for b in range(3):
-                piece = field[(start + a) * cols : (start + a + count) * cols, b * ch : (b + 1) * ch]
-                part = lax.dot_general(
-                    piece, weight[2 - a, (2 - b) * ch : (3 - b) * ch, :],
-                    (((1,), (1,)), ((), ())), preferred_element_type=F32,
+                target[a, b * ch : (b + 1) * ch, :] = source[2 - a, (2 - b) * ch : (3 - b) * ch, :].T
+
+    def centre(field, weight, start, count, steps):
+        total = None
+        for a in steps:
+            piece = field[(start + a) * cols : (start + a + count) * cols, mid]
+            part = jnp.dot(piece, weight[a, mid, :], preferred_element_type=F32)
+            total = part if total is None else total + part
+        partial[start * cols : (start + count) * cols, :] = total
+
+    def centres(field, weight):
+        for start in range(0, rows, group):
+            steps = (1, 2) if start == 0 else (0, 1) if start == rows - group else (0, 1, 2)
+            centre(field, weight, start, group, steps)
+
+    def conv_rest(field, weight, start, count):
+        total = partial[start * cols : (start + count) * cols, :]
+        for a in range(3):
+            where = slice((start + a) * cols, (start + a + count) * cols)
+            for b in (0, 2):
+                lanes_b = slice(b * ch, (b + 1) * ch)
+                total = total + jnp.dot(
+                    field[where, lanes_b], weight[a, lanes_b, :], preferred_element_type=F32
                 )
-                total = part if total is None else total + part
+        if start in (0, rows - group):
+            a = 0 if start == 0 else 2
+            where = slice((start + a) * cols, (start + a + count) * cols)
+            total = total + jnp.dot(field[where, mid], weight[a, mid, :], preferred_element_type=F32)
         return total
 
-    def put_rows(field, start, count, value):
+    def put_rows(field, start, count, value, sides):
         for k in range(count):
-            put_row(field, start + 1 + k, value[k * cols : (k + 1) * cols])
-
-    def middle(step):
-        for start in range(group, rows - group, MID):
-            step(start, MID)
-
-    def outer(step):
-        step(0, group)
-        step(rows - group, group)
+            part = value[k * cols : (k + 1) * cols]
+            put_mid(field, start + 1 + k, part)
+            if sides:
+                put_sides(field, start + 1 + k, part)
+
+    def middle(step, block):
+        for start in range(group, rows - group, block):
+            step(start, block)
+
+    def outer(step, block):
+        for base in (0, rows - group):
+            for start in range(base, base + group, block):
+                step(start, block)
 
     own_rows = pl.ds(pl.multiple_of(core * half, half), half)
     other_rows = pl.ds(pl.multiple_of((1 - core) * half, half), half)
@@ -264,11 +295,11 @@
 
     def finish(piece):
         last_copy(piece).wait()
-        out = (o2_ref, o1_ref)[piece[0]]
-        for c in range(2):
-            out[taps(piece), :, c * half : (c + 1) * half] = final[piece[0], c, taps(piece)]
-
-    early, late = pieces[:3], [pieces[3 + 3 * a : 6 + 3 * a] for a in range(3)]
+        if piece[0] == 0:
+            for c in range(2):
+                o2_ref[taps(piece), :, c * half : (c + 1) * half] = final[0, c, taps(piece)].astype(F32)
+
+    early, late = pieces[:3], pieces[3:]
 
     def each(step, some):
         for piece in some:
@@ -282,104 +313,118 @@
     send(0, xs)
 
     def load(row, carry):
-        put_row(xs, row + 1, in_ref[row].astype(F32), mark=False)
+        value = in_ref[row].astype(F32)
+        put_mid(xs, row + 1, value, mark=False)
+        put_sides(xs, row + 1, value)
         return carry
 
     lax.fori_loop(0, rows, load, 0)
-    loads[1].wait()
+    for copy in loads[1:]:
+        copy.wait()
+    flip(w1_ref, wt1)
+    flip(w2_ref, wt2)
 
     def span(start, count):
         return slice(start * cols, (start + count) * cols)
 
     def first(start, count):
-        value = conv(xs, w1_ref, start, count)
-        part, slope = slope_parts(value)
-        slope1[span(start, count), :] = slope
-        put_rows(acts, start, count, value * part)
-
+        value = conv_rest(xs, w1_ref, start, count)
+        slope1[span(start, count), :] = value
+        put_rows(acts, start, count, value * half_erf(value), False)
+
+    centres(xs, w1_ref)
     receive_sides(0, xs)
-    middle(first)
+    middle(first, B1)
     receive_ends(0, xs)
-    outer(first)
+    outer(first, B1)
     send(1, acts)
-    loads[2].wait()
-    loads[3].wait()
+
+    def fill(row, carry):
+        where = pl.ds(pl.multiple_of(row * cols, cols), cols)
+        slope1[where, :] = slope_of(slope1[where, :])
+        put_sides(acts, row + 1, acts[line(row + 1), mid].astype(F32))
+        return carry
+
+    lax.fori_loop(0, rows, fill, 0)
 
     def second(start, count):
-        value = conv(acts, w2_ref, start, count)
-        _, slope = slope_parts(value)
+        value = conv_rest(acts, w2_ref, start, count)
         rate = cot_ref[start : start + count].astype(F32).reshape(count * cols, ch)
-        delta = rate * slope
-        put_rows(d2s, start, count, delta)
-        turned[:, span(start, count)] = delta.T.astype(BF16)
-
+        delta = rate * slope_of(value)
+        put_rows(d2s, start, count, delta, True)
+        turned[:, span(start, count)] = delta.astype(BF16).T
+
+    centres(acts, w2_ref)
     receive_sides(1, acts)
-    middle(second)
+    middle(second, B2)
     receive_ends(1, acts)
-    outer(second)
+    outer(second, B2)
     send(2, d2s)
     grad_piece(0, 0, acts)
     grad_piece(0, 1, acts)
+    grad_piece(0, 2, acts)
     scatter(early[0])
-    grad_piece(0, 2, acts)
 
     def third(start, count):
-        value = conv_t(d2s, w2_ref, start, count)
+        value = conv(d2s, wt2, start, count)
         delta = value * slope1[span(start, count), :]
-        put_rows(d1s, start, count, delta)
-        turned[:, span(start, count)] = delta.T.astype(BF16)
+        put_rows(d1s, start, count, delta, False)
+        turned[:, span(start, count)] = delta.astype(BF16).T
 
     receive_sides(2, d2s)
-    middle(third)
-    each(scatter, early[1:])
+    middle(third, B3)
+    scatter(early[1])
+    scatter(early[2])
     receive_ends(2, d2s)
-    outer(third)
+    outer(third, B3)
     send(3, d1s)
     grad_piece(1, 0, xs)
     grad_piece(1, 1, xs)
-    each(scatter, late[0])
+    each(scatter, late[:3])
     depth(early[0])
     grad_piece(1, 2, xs)
-    each(scatter, late[1])
+    each(scatter, late[3:6])
+    depth(early[1])
+    each(scatter, late[6:])
+    for row in range(1, rows + 1):
+        put_sides(d1s, row, d1s[line(row), mid].astype(F32))
 
     def fourth(start, count):
-        value = conv_t(d1s, w1_ref, start, count)
+        value = conv(d1s, wt1, start, count)
         dx_ref[start : start + count] = value.astype(BF16).reshape(count, cols, ch)
 
     receive_sides(3, d1s)
-    middle(fourth)
-    each(scatter, late[2])
-    depth(early[1])
+    depth(early[2])
+    middle(fourth, B4)
     receive_ends(3, d1s)
-    outer(fourth)
-    depth(early[2])
-    each(depth, late[0])
+    outer(fourth, B4)
+    each(depth, late[:3])
     spread(early[0])
-    each(depth, late[1])
+    each(depth, late[3:6])
     spread(early[1])
-    each(depth, late[2])
+    each(depth, late[6:])
     spread(early[2])
-    each(spread, late[0])
-    join(early[0])
-    each(spread, late[1])
-    join(early[1])
-    each(spread, late[2])
-    join(early[2])
+    each(spread, late)
+    each(join, early)
+    each(join, late[:3])
     each(finish, early)
-    for some in late:
-        each(join, some)
-    for some in late:
-        each(finish, some)
-
-
-def write_kernel(dx_ref, g1_ref, g2_ref, dx_out, o1_out, o2_out, wide, sems):
-    copies = [pltpu.make_async_copy(dx_ref, dx_out, sems.at[18])]
-    copies[0].start()
-    for n, (ref, out) in enumerate(((g1_ref, o1_out), (g2_ref, o2_out))):
-        for t in range(9):
-            wide[n, t] = ref[t].astype(F32)
-            copies.append(pltpu.make_async_copy(wide.at[n, t], out.at[t], sems.at[9 * n + t]))
-            copies[-1].start()
+    each(join, late[3:])
+    each(finish, late)
+
+
+def write_kernel(dx_ref, final, g2_ref, dx_out, o1_out, o2_out, wide, sems):
+    half = final.shape[-1]
+    copies = [
+        pltpu.make_async_copy(g2_ref, o2_out, sems.at[9]),
+        pltpu.make_async_copy(dx_ref, dx_out, sems.at[10]),
+    ]
+    for copy in copies:
+        copy.start()
+    for t in range(9):
+        for c in range(2):
+            wide[t, :, c * half : (c + 1) * half] = final[1, c, t].astype(F32)
+        copies.append(pltpu.make_async_copy(wide.at[t], o1_out.at[t], sems.at[t]))
+        copies[-1].start()
     for copy in copies:
         copy.wait()
 
@@ -393,12 +438,12 @@
     half = ch // 2
     padded = pltpu.VMEM(((rows + 2) * cols, 3 * ch), BF16)
     dma = pltpu.SemaphoreType.DMA
-    dx, o1, o2 = pl.pallas_call(
+    dx, final, o2 = pl.pallas_call(
         functools.partial(kernel, lats, lons, rows, cols, ch, group),
         out_shape=(
             jax.ShapeDtypeStruct((rows, cols, ch), BF16),
-            jax.ShapeDtypeStruct((9, ch, ch), BF16),
-            jax.ShapeDtypeStruct((9, ch, ch), BF16),
+            jax.ShapeDtypeStruct((2, 2, 9, ch, half), BF16),
+            jax.ShapeDtypeStruct((9, ch, ch), F32),
         ),
         in_specs=[hbm] * 4,
         out_specs=(vmem,) * 3,
@@ -407,7 +452,10 @@
             pltpu.VMEM((3, 3 * ch, ch), BF16),
             pltpu.VMEM((3, 3 * ch, ch), BF16),
             pltpu.VMEM((rows, cols, ch), BF16),
+            pltpu.VMEM((3, 3 * ch, ch), BF16),
+            pltpu.VMEM((3, 3 * ch, ch), BF16),
             padded, padded, padded, padded,
+            pltpu.VMEM((cells, ch), F32),
             pltpu.VMEM((cells, ch), F32),
             pltpu.VMEM((ch, cells), BF16),
             pltpu.VMEM((2, rows, ch), F32),
@@ -420,7 +468,6 @@
             pltpu.VMEM((2, 9, ch, half), BF16),
             pltpu.VMEM((2, 9, 15, 16, half), BF16),
             pltpu.VMEM((2, 9, 8, 16, half), BF16),
-            pltpu.VMEM((2, 2, 9, ch, half), BF16),
             dma((4,)), dma((4, 8)), dma((4, 8)),
             dma((12, 2)), dma((12, 2)), dma((12, 2)), dma((12, 2)), dma((12, 2)),
         ],
@@ -448,10 +495,10 @@
         ),
         in_specs=[vmem] * 3,
         out_specs=(hbm,) * 3,
-        scratch_shapes=[pltpu.VMEM((2, 9, ch, ch), F32), dma((19,))],
+        scratch_shapes=[pltpu.VMEM((9, ch, ch), F32), dma((11,))],
         compiler_params=pltpu.CompilerParams(vmem_limit_bytes=12 * 1024 * 1024),
         name="write",
-    )(dx, o1, o2)
+    )(dx, final, o2)
     return dx, o1.reshape(3, 3, ch, ch), o2.reshape(3, 3, ch, ch)
 
 

time: 65.8 us -> 63.7 us (0.968)
  Pallas kernels: 64.9 us -> 62.8 us
    pallas_call x1, Pallas kernels: 62.3 us -> 60.3 us  [body(): pl.pallas_call(functools.partial(kernel, lats, lons, rows, cols, ch, grou...]
where the time goes in v4:
time: 63.7 us; the launch traced here: 63.6 us
  Pallas kernels  62.8 us (99%)
  between operations  0.8 us (1%)
    pallas_call x1, Pallas kernels, body(): pl.pallas_call(functools.partial(kernel, lats, lons, rows, cols, ch, grou...  60.3 us
    pallas_call x1, Pallas kernels, body(): pl.pallas_call(write_kernel, out_shape=(jax.ShapeDtypeStruct((rows, cols,...  2.49 us

profile of v4, /device:TPU:1, one launch (start us, length us, event | category | flops | bytes accessed | tf_op | source)
XLA Modules:
  0.0 63.6 jit_solution(6474755096669193810)
XLA Ops:
  0.6 60.3 %stages.1 = (bf16[16,96,256]{2,1,0:T(8,128)(2,1)S(1)}, bf16[2,2,9,256,128]{4,3,2,1,0:T(8,128)(2,1)S(1)}, f32[9,256,256]{2,1,0:T(8,128)S(1)}) custom-call(bf16[16,96,256]{2,1,0:T(8,128)(2,1)} %in_hbm.1, bf16[3,768,256]{2,1,0:T(8,128)(2,1)} %bitcast.4, bf16[3,768,256]{2,1,0:T(8,128)(2,1)} %bitcast.5, bf16[16,96,256]{2,1,0:T(8,128)(2,1)} %cot_hbm.1), custom_call_target="tpu_custom_call" | custom-call | tf_op jit(solution)/shard_map/stages/pallas_call | solution.py:441
  61.0 2.5 %write.1 = (bf16[16,96,256]{2,1,0:T(8,128)(2,1)}, f32[9,256,256]{2,1,0:T(8,128)}, f32[9,256,256]{2,1,0:T(8,128)}) custom-call(bf16[16,96,256]{2,1,0:T(8,128)(2,1)S(1)} %get-tuple-element.9.dx_ref, bf16[2,2,9,256,128]{4,3,2,1,0:T(8,128)(2,1)S(1)} %get-tuple-element.10.final, f32[9,256,256]{2,1,0:T(8,128)S(1)} %get-tuple-element.11.g2_ref), custom_call_target="tpu_custom_call" | custom-call | tf_op jit(solution)/shard_map/write/pallas_call | solution.py:489

commit v5 on v4

--- a/solution.py
+++ b/solution.py
@@ -239,9 +239,10 @@
         pltpu.make_async_copy(ref, ref, sems.at[1]).wait()
 
     def grad_piece(g, a, field):
-        grads[g, a] = jnp.dot(
-            turned[...], field[a * cols : (a + rows) * cols, :], preferred_element_type=F32
-        )
+        for part in (slice(0, half), slice(half, ch)):
+            grads[g, a, part, :] = jnp.dot(
+                turned[part, :], field[a * cols : (a + rows) * cols, :], preferred_element_type=F32
+            )
         for piece in pieces:
             if piece[0] == g and piece[1] // 3 == a:
                 pair_copy(piece).start()

time: 63.7 us -> 63.3 us (level)
  no operation moved by 1% of the time
where the time goes in v5:
time: 63.3 us; the launch traced here: 63.2 us
  Pallas kernels  62.4 us (99%)
  between operations  0.8 us (1%)
    pallas_call x1, Pallas kernels, body(): pl.pallas_call(functools.partial(kernel, lats, lons, rows, cols, ch, grou...  59.9 us
    pallas_call x1, Pallas kernels, body(): pl.pallas_call(write_kernel, out_shape=(jax.ShapeDtypeStruct((rows, cols,...  2.49 us

profile of v5, /device:TPU:1, one launch (start us, length us, event | category | flops | bytes accessed | tf_op | source)
XLA Modules:
  0.0 63.2 jit_solution(1576909143975585843)
XLA Ops:
  0.6 59.9 %stages.1 = (bf16[16,96,256]{2,1,0:T(8,128)(2,1)S(1)}, bf16[2,2,9,256,128]{4,3,2,1,0:T(8,128)(2,1)S(1)}, f32[9,256,256]{2,1,0:T(8,128)S(1)}) custom-call(bf16[16,96,256]{2,1,0:T(8,128)(2,1)} %in_hbm.1, bf16[3,768,256]{2,1,0:T(8,128)(2,1)} %bitcast.4, bf16[3,768,256]{2,1,0:T(8,128)(2,1)} %bitcast.5, bf16[16,96,256]{2,1,0:T(8,128)(2,1)} %cot_hbm.1), custom_call_target="tpu_custom_call" | custom-call | tf_op jit(solution)/shard_map/stages/pallas_call | solution.py:442
  60.6 2.5 %write.1 = (bf16[16,96,256]{2,1,0:T(8,128)(2,1)}, f32[9,256,256]{2,1,0:T(8,128)}, f32[9,256,256]{2,1,0:T(8,128)}) custom-call(bf16[16,96,256]{2,1,0:T(8,128)(2,1)S(1)} %get-tuple-element.9.dx_ref, bf16[2,2,9,256,128]{4,3,2,1,0:T(8,128)(2,1)S(1)} %get-tuple-element.10.final, f32[9,256,256]{2,1,0:T(8,128)S(1)} %get-tuple-element.11.g2_ref), custom_call_target="tpu_custom_call" | custom-call | tf_op jit(solution)/shard_map/write/pallas_call | solution.py:490
